TPU v7x, 32 devices: a whole 2x2x4 slice. The times are simulated.
32 devices in a mesh: level: 8 (over z, core), member: 4 (over y, x).
Axes of the slice: x: 2, y: 2, z: 4, core: 2. Of those that a mesh axis runs over, the one named last changes fastest.
Arguments:
- model_state: float32 [4, 32, 4, 256, 512], P('member', 'level'), may hold values from -6 to 6
- noise_field: bfloat16 [4, 32, 4, 256, 512], P('member', 'level'), may hold values from -5 to 5
- cotangent: bfloat16 [4, 32, 4, 256, 512], P('member', 'level'), may hold values from -6 to 6
- zonal_shift: float32 [32, 4], P('level'), may hold values from -0.02 to 0.02
- viscosity: float32 [32, 4], P('level'), may hold values from 0.1 to 3
- noise_scale: float32 [32, 4], P('level'), may hold values from 0.2 to 1
- w_in: bfloat16 [128, 384], replicated, may hold values from -0.5 to 0.5
- b_in: float32 [384], replicated, may hold values from -3 to 3
- w_mid: bfloat16 [384, 384], replicated, may hold values from -0.3125 to 0.3125
- b_mid: float32 [384], replicated, may hold values from -3 to 3
- w_out: bfloat16 [384, 128], replicated, may hold values from -0.3125 to 0.3125
Outputs:
- next_state: float32 [4, 32, 4, 256, 512], P('member', 'level')
- state_grad: float32 [4, 32, 4, 256, 512], P('member', 'level')
- grad_w_in: float32 [128, 384], P(None, ('level', 'member'))
- grad_w_mid: float32 [384, 384], P(None, ('level', 'member'))
- grad_w_out: float32 [128, 384], P(None, ('level', 'member'))
- grad_bias: float32 [2, 384], P(None, ('level', 'member'))
All inputs are finite; a program needn't handle non-finite values.
Results may differ from a plain program's by a relative error of at most 0.0085.
Values may be sent and summed in bfloat16 or wider, within the bound.
No kernel may reach another device: no remote copies, remote signals or barrier semaphores. Data moves between devices by JAX's collectives and lax.ppermute only.
A program may use at most 192 MiB of HBM per device.

v0:
```python
import math

import jax
import jax.numpy as jnp
import numpy as np
from jax import lax
from jax.experimental import pallas as pl
from jax.experimental.pallas import tpu as pltpu
from jax.sharding import PartitionSpec as P


WAVES = 128
MODES = 128
BF = jnp.bfloat16
F32 = jnp.float32


def dot(a, b):
    return lax.dot_general(a, b, (((1,), (0,)), ((), ())), preferred_element_type=F32)


def dot_t(a, b):
    return lax.dot_general(a, b, (((1,), (1,)), ((), ())), preferred_element_type=F32)


def split(x):
    hi = x.astype(BF)
    return hi, (x - hi.astype(F32)).astype(BF)


def dot3(a, b):
    return dot(a[0], b[0]) + (dot(a[1], b[0]) + dot(a[0], b[1]))


def host_split(table):
    table = table.astype(np.float32)
    hi = table.astype(BF)
    lo = (table - hi.astype(np.float32)).astype(BF)
    return np.ascontiguousarray(hi), np.ascontiguousarray(lo)


def spectral_tables(lat_count, lon_count):
    turn = (np.arange(lon_count)[:, None] * np.arange(WAVES)[None, :]) % lon_count
    angle = 2.0 * np.pi * turn / lon_count
    lon = np.concatenate([np.cos(angle), np.sin(angle)], axis=1)
    lat = np.cos(np.pi * (np.arange(lat_count)[:, None] + 0.5) * np.arange(MODES)[None, :] / lat_count)
    return lon, lat


def rotation_rows(zonal_shift, viscosity, lat_count, lon_count):
    shift = zonal_shift.reshape(-1, 1, 1)
    visc = viscosity.reshape(-1, 1, 1)
    wave = jnp.arange(WAVES, dtype=F32)
    mode = jnp.arange(MODES, dtype=F32)
    wave_scale = jnp.where(wave == 0, 1.0, 2.0) / lon_count
    mode_scale = jnp.where(mode == 0, 1.0, 2.0) / lat_count
    damp_k = (jnp.exp(-visc * ((wave / WAVES) ** 2)[None, None, :]) * wave_scale)
    cosine = jnp.cos(shift * wave[None, None, :]) * damp_k
    sine = jnp.sin(shift * wave[None, None, :]) * damp_k
    damp_p = jnp.exp(-visc * ((mode / MODES) ** 2)[None, :, None]) * mode_scale[None, :, None]
    return cosine, sine, damp_p


def rotate(spec, cos_ref, sin_ref, damp_ref, sign):
    cosine = cos_ref[0]
    sine = sin_ref[0] * sign
    a = spec[:, :WAVES] * damp_ref[0]
    b = spec[:, WAVES:] * damp_ref[0]
    return jnp.concatenate([a * cosine - b * sine, a * sine + b * cosine], axis=1)


def pair(h_ref, l_ref):
    return h_ref[...], l_ref[...]


def spectral_fwd_kernel(x_ref, c_ref, s_ref, d_ref, fh, fl, fth, ftl, ah, al, ath, atl, half_ref, dyn_ref):
    z = dot3(split(x_ref[0]), pair(fh, fl))
    spec = dot3(pair(ath, atl), split(z))
    rot = rotate(spec, c_ref, s_ref, d_ref, 1.0)
    half = split(dot3(pair(ah, al), split(rot)))
    half_ref[0] = half[0]
    dyn_ref[0] = dot3(half, pair(fth, ftl))


def cot_spec_kernel(x_ref, fh, fl, ath, atl, out_ref):
    x = x_ref[0]
    z = dot(x, fh[...]) + dot(x, fl[...])
    out_ref[0] = dot3(pair(ath, atl), split(z))


def spectral_bwd_kernel(b_ref, g_ref, c_ref, s_ref, d_ref, fth, ftl, ah, al, ath, atl, out_ref):
    b = b_ref[0]
    spec = dot(ath[...], b) + dot(atl[...], b) + g_ref[0]
    rot = rotate(spec, c_ref, s_ref, d_ref, -1.0)
    half = split(dot3(pair(ah, al), split(rot)))
    out_ref[0] = dot3(half, pair(fth, ftl))


def grad_tend_kernel(noise_ref, cot_ref, ns_ref, out_ref):
    factor = 1.0 + ns_ref[...] * noise_ref[...].astype(F32)
    out_ref[0] = jnp.swapaxes(cot_ref[...].astype(F32) * factor, 0, 1).astype(BF)


def next_state_kernel(tend_ref, dyn_ref, noise_ref, ns_ref, *rest):
    out_ref = rest[-1]
    factor = 1.0 + ns_ref[...] * noise_ref[...].astype(F32)
    tend = jnp.swapaxes(tend_ref[0].astype(F32), 0, 1)
    out_ref[...] = dyn_ref[...] + tend * factor


def sigmoid(x):
    return 0.5 * jnp.tanh(0.5 * x) + 0.5


def gather_rows(ref, rows):
    parts = []
    for row in range(rows):
        v = ref[:, row]
        parts.append(v.reshape(v.shape[0] * v.shape[1], v.shape[2]))
    return parts


def inputs_of(half_ref, fth, ftl, rows):
    parts = []
    for h in gather_rows(half_ref, rows):
        parts.append((dot(h, fth[...]) + dot(h, ftl[...])).astype(BF))
    return jnp.concatenate(parts, axis=1)


def columns_fwd_kernel(half_ref, fth, ftl, w_in_t, b_in, w_mid_t, b_mid, w_out_t, out_ref):
    groups, rows, per_group, lon_count = out_ref.shape
    inputs = inputs_of(half_ref, fth, ftl, rows)
    pre_one = dot(w_in_t[...], inputs) + b_in[...]
    act_one = (pre_one * sigmoid(pre_one)).astype(BF)
    pre_two = dot(w_mid_t[...], act_one) + b_mid[...]
    act_two = (pre_two * sigmoid(pre_two)).astype(BF)
    tend = dot(w_out_t[...], act_two).astype(BF)
    for row in range(rows):
        part = tend[:, row * lon_count : (row + 1) * lon_count]
        out_ref[:, row] = part.reshape(groups, per_group, lon_count)


def lane_sums(x):
    total = x[:, :128]
    for at in range(128, x.shape[1], 128):
        total = total + x[:, at : at + 128]
    return total


def columns_bwd_kernel(
    half_ref, grad_ref, acc_in, bias_in, fth, ftl, fh, w_in_t, b_in, w_mid_t, b_mid, w_in, w_mid, w_out, *rest
):
    back_ref, acc_ref, bias_ref = rest[-3:]
    groups, rows, per_group, lon_count = grad_ref.shape
    ein = w_in.shape[0]
    hid = w_mid.shape[0]

    @pl.when(pl.program_id(0) == 0)
    def _():
        acc_ref[...] = acc_in[...]
        bias_ref[...] = bias_in[...]

    inputs = inputs_of(half_ref, fth, ftl, rows)
    grad = jnp.concatenate(gather_rows(grad_ref, rows), axis=1)
    pre_one = dot(w_in_t[...], inputs) + b_in[...]
    sig_one = sigmoid(pre_one)
    full_one = pre_one * sig_one
    act_one = full_one.astype(BF)
    silu_one = sig_one + full_one * (1.0 - sig_one)
    pre_two = dot(w_mid_t[...], act_one) + b_mid[...]
    sig_two = sigmoid(pre_two)
    full_two = pre_two * sig_two
    act_two = full_two.astype(BF)
    slope_two_f = dot(w_out[...], grad) * (sig_two + full_two * (1.0 - sig_two))
    slope_two = slope_two_f.astype(BF)
    slope_one_f = dot(w_mid[...], slope_two) * silu_one
    slope_one = slope_one_f.astype(BF)
    bias_ref[:, :128] += lane_sums(slope_one_f)
    bias_ref[:, 128:] += lane_sums(slope_two_f)
    acc_ref[:, :ein] += dot_t(slope_one, inputs)
    acc_ref[:, ein : ein + hid] += dot_t(slope_two, act_one)
    acc_ref[:, ein + hid :] += dot_t(act_two, grad)
    back = dot(w_in[...], slope_one).astype(BF)
    for row in range(rows):
        part = back[:, row * lon_count : (row + 1) * lon_count]
        out = dot(part, fh[...]).astype(BF)
        back_ref[:, row] = out.reshape(groups, per_group, out.shape[1])


def whole_spec(shape):
    return pl.BlockSpec(shape, lambda *_: (0,) * len(shape))


def call(kernel, grid, in_specs, out_specs, out_shape, flops, args, aliases=None):
    return pl.pallas_call(
        kernel,
        grid=grid,
        in_specs=in_specs,
        out_specs=out_specs,
        out_shape=out_shape,
        input_output_aliases=aliases or {},
        cost_estimate=pl.CostEstimate(flops=flops, transcendentals=0, bytes_accessed=1 << 22),
        compiler_params=pltpu.CompilerParams(
            dimension_semantics=("arbitrary",) * len(grid), vmem_limit_bytes=56 << 20
        ),
    )(*args)


def per_device(
    model_state, noise_field, cotangent, zonal_shift, viscosity, noise_scale, w_in, b_in, w_mid, b_mid, w_out
):
    members_here, levels, fields, nlat, nlon = model_state.shape
    groups = lax.axis_size("level")
    members = lax.axis_size("member")
    lf = levels * fields
    own = nlat // groups
    part = own // 2
    ein, hid = w_in.shape
    state = model_state.reshape(lf, nlat, nlon)
    noise = noise_field.reshape(lf, nlat, nlon)
    cot = cotangent.reshape(lf, nlat, nlon)
    scale = noise_scale.reshape(lf, 1, 1)
    lon, lat = spectral_tables(nlat, nlon)
    fh, fl = host_split(lon)
    fth, ftl = host_split(lon.T)
    ah, al = host_split(lat)
    ath, atl = host_split(lat.T)
    waves2 = fh.shape[1]

    def sds(shape, dtype):
        return jax.ShapeDtypeStruct(shape, dtype)

    def grad_part(which):
        at = pl.BlockSpec((lf, part, nlon), lambda s: (0, 2 * s + which, 0))
        return call(
            grad_tend_kernel,
            (groups,),
            [at, at, whole_spec((lf, 1, 1))],
            pl.BlockSpec((1, part, lf, nlon), lambda s: (s, 0, 0, 0)),
            sds((groups, part, lf, nlon), BF),
            10**9,
            (noise, cot, scale),
        )

    def exchange(x, axis="level"):
        return lax.all_to_all(x, axis, split_axis=0, concat_axis=0, tiled=True)

    per_lf = lambda *shape: pl.BlockSpec((1,) + shape, lambda s: (s,) + (0,) * len(shape))
    row_spec = per_lf(1, WAVES)
    col_spec = per_lf(MODES, 1)
    f_specs = [whole_spec(fh.shape)] * 2
    ft_specs = [whole_spec(fth.shape)] * 2
    a_specs = [whole_spec(ah.shape)] * 2
    at_specs = [whole_spec(ath.shape)] * 2

    def ordered(value, *after):
        return lax.optimization_barrier((value,) + after)[0]

    grad_one_send = grad_part(0)
    grad_one = exchange(grad_one_send)
    state, shift, visc, _ = lax.optimization_barrier((state, zonal_shift, viscosity, grad_one_send))
    cosine, sine, damp_p = rotation_rows(shift, visc, nlat, nlon)
    half, dyn = call(
        spectral_fwd_kernel,
        (lf,),
        [per_lf(nlat, nlon), row_spec, row_spec, col_spec] + f_specs + ft_specs + a_specs + at_specs,
        [per_lf(nlat, waves2), per_lf(nlat, nlon)],
        [sds((lf, nlat, waves2), BF), sds((lf, nlat, nlon), F32)],
        2 * 10**10,
        (state, cosine, sine, damp_p, fh, fl, fth, ftl, ah, al, ath, atl),
    )
    send = half.reshape(lf, groups, own, waves2).transpose(1, 2, 0, 3)
    cols = exchange(ordered(send, grad_one))
    grad_two_send = grad_part(1)
    grad_two = exchange(ordered(grad_two_send, cols))
    cot_spec = call(
        cot_spec_kernel,
        (lf,),
        [per_lf(nlat, nlon)] + f_specs + at_specs,
        per_lf(MODES, waves2),
        sds((lf, MODES, waves2), F32),
        10**10,
        (cot, fh, fl, ath, atl),
    )

    w_in_t = w_in.T
    w_mid_t = w_mid.T
    w_out_t = w_out.T
    bias_one = b_in.reshape(hid, 1)
    bias_two = b_mid.reshape(hid, 1)
    step = 2
    steps = part // step

    def half_spec(which):
        return pl.BlockSpec((groups, step, lf, waves2), lambda s: (0, s + which * steps, 0, 0))

    grid_spec = pl.BlockSpec((groups, step, lf, nlon), lambda s: (0, s, 0, 0))

    def forward(which):
        return call(
            columns_fwd_kernel,
            (steps,),
            [half_spec(which)]
            + ft_specs
            + [whole_spec(v.shape) for v in (w_in_t, bias_one, w_mid_t, bias_two, w_out_t)],
            grid_spec,
            sds((groups, part, lf, nlon), BF),
            10**10,
            (cols, fth, ftl, w_in_t, bias_one, w_mid_t, bias_two, w_out_t),
        )

    acc_shape = (hid, 2 * ein + hid)
    sums_shape = (hid, 256)

    def backward(which, grads, acc, sums, before):
        specs = (
            [half_spec(which), grid_spec, whole_spec(acc_shape), whole_spec(sums_shape)]
            + ft_specs
            + [whole_spec(fh.shape)]
            + [whole_spec(v.shape) for v in (w_in_t, bias_one, w_mid_t, bias_two, w_in, w_mid, w_out)]
        )
        args = (cols, grads, acc, sums, fth, ftl, fh, w_in_t, bias_one, w_mid_t, bias_two, w_in, w_mid, w_out)
        aliases = {}
        if before is not None:
            aliases = {len(args): 0}
            specs = specs + [pl.BlockSpec(memory_space=pl.ANY)]
            args = args + (before,)
        return call(
            columns_bwd_kernel,
            (steps,),
            specs,
            [half_spec(which), whole_spec(acc_shape), whole_spec(sums_shape)],
            [sds((groups, own, lf, waves2), BF), sds(acc_shape, F32), sds(sums_shape, F32)],
            3 * 10**10,
            args,
            aliases,
        )

    tend_one_send = forward(0)
    tend_one = exchange(ordered(tend_one_send, grad_two))
    back, acc, sums = backward(0, grad_one, jnp.zeros(acc_shape, F32), jnp.zeros(sums_shape, F32), None)
    tend_two_send = forward(1)
    back, acc, sums = backward(1, grad_two, acc, sums, back)
    back = exchange(ordered(back, tend_one))

    def reduce_axis(x, axis):
        size = lax.axis_size(axis)
        at = lax.axis_index(axis)
        total = lax.dynamic_index_in_dim(x, at, 0, keepdims=False)
        for hop in range(1, size):
            block = lax.dynamic_index_in_dim(x, (at + hop) % size, 0, keepdims=False)
            total = total + lax.ppermute(block, axis, [(s, (s + hop) % size) for s in range(size)])
        return total

    sums_two = jnp.stack([jnp.sum(sums[:, :128], axis=1), jnp.sum(sums[:, 128:], axis=1)], axis=1)
    packed = jnp.concatenate([acc, sums_two], axis=1)
    width = packed.shape[1]
    share = hid // (groups * members)
    packed = packed.reshape(groups, members, share, width).transpose(1, 0, 2, 3)
    packed = reduce_axis(packed, "member")
    packed = reduce_axis(packed, "level")
    packed = packed * (1.0 / math.sqrt(members_here * members * nlat * nlon))
    packed = packed.T
    tend_two = exchange(ordered(tend_two_send, back, packed))

    def finish(which, tend, before):
        rows = pl.BlockSpec((lf, part, nlon), lambda s: (0, 2 * s + which, 0))
        specs = [pl.BlockSpec((1, part, lf, nlon), lambda s: (s, 0, 0, 0)), rows, rows, whole_spec((lf, 1, 1))]
        args = (tend, dyn, noise, scale)
        aliases = {}
        if before is not None:
            aliases = {len(args): 0}
            specs = specs + [pl.BlockSpec(memory_space=pl.ANY)]
            args = args + (before,)
        return call(
            next_state_kernel, (groups,), specs, rows, sds((lf, nlat, nlon), F32), 10**10, args, aliases
        )

    next_state = finish(0, tend_one, None)
    state_grad = call(
        spectral_bwd_kernel,
        (lf,),
        [per_lf(nlat, waves2), per_lf(MODES, waves2), row_spec, row_spec, col_spec]
        + ft_specs
        + a_specs
        + at_specs,
        per_lf(nlat, nlon),
        sds((lf, nlat, nlon), F32),
        2 * 10**10,
        (
            back.reshape(nlat, lf, waves2).transpose(1, 0, 2),
            cot_spec, cosine, sine, damp_p, fth, ftl, ah, al, ath, atl,
        ),
    )
    next_state = finish(1, tend_two, next_state)

    shape = model_state.shape
    return (
        next_state.reshape(shape),
        state_grad.reshape(shape),
        packed[:ein],
        packed[ein : ein + hid],
        packed[ein + hid : 2 * ein + hid],
        packed[2 * ein + hid :],
    )


def solution(mesh):
    big = P("member", "level", None, None, None)
    small = P("level", None)
    grads = P(None, ("level", "member"))
    return jax.shard_map(
        per_device,
        mesh=mesh,
        in_specs=(big, big, big, small, small, small, P(), P(), P(), P(), P()),
        out_specs=(big, big, grads, grads, grads, grads),
        check_vma=False,
    )
```

profile of v0, /device:TPU:0, one launch (start us, length us, event | category | flops | bytes accessed | tf_op | source)
XLA Modules:
  0.0 369.5 jit_solution(6094443960515567297)
XLA Ops:
  2.0 6.9 %shard_map.226 = bf16[8,16,16,512]{3,2,1,0:T(8,128)(2,1)} custom-call(bf16[16,256,512]{2,1,0:T(8,128)(2,1)} %bitcast.74, bf16[16,256,512]{2,1,0:T(8,128)(2,1)} %bitcast.71, f32[16,1,1]{2,1,0:T(1,128)} %reshape.396.ns_ref), custom_call_target="tpu_custom_call" | custom-call | flops 1000000000 | bytes 4194304 | tf_op jit(solution)/shard_map/pallas_call | solution.py:195
  8.9 6.5 %all-to-all-start = ((bf16[8,16,16,512]{3,2,1,0:T(8,128)(2,1)}), bf16[8,16,16,512]{3,2,1,0:T(8,128)(2,1)S(1)}, u32[]{:S(2)}, u32[]{:S(2)}) async-start(bf16[8,16,16,512]{3,2,1,0:T(8,128)(2,1)} %shard_map.226), calls=%async_computation | async-start | bytes 4194304 | tf_op jit(solution)/shard_map/all_to_all | solution.py:246
  17.8 27.1 %shard_map.227 = (bf16[16,256,256]{2,1,0:T(8,128)(2,1)}, f32[16,256,512]{2,1,0:T(8,128)}) custom-call(f32[16,256,512]{2,1,0:T(8,128)} %bitcast.98, f32[16,1,128]{2,1,0:T(1,128)} %get-tuple-element.79.c_ref, f32[16,1,128]{2,1,0:T(1,128)} %get-tuple-element.78.s_ref, f32[16,128,1]{2,1,0:T(8,128)} %exponential_multiply_fusion.d_ref, ...), custom_call_target="tpu_custom_call" | custom-call | flops 20000000000 | bytes 4194304 | tf_op jit(solution)/shard_map/pallas_call | solution.py:195
  44.9 4.1 %copy.92 = bf16[16,256,256]{2,0,1:T(8,128)(2,1)} copy(bf16[16,256,256]{2,1,0:T(8,128)(2,1)} %get-tuple-element.25) | data formatting | bytes 4194304 | tf_op jit(solution)/shard_map/pallas_call | solution.py:195
  49.0 15.4 %all-to-all-done.grad_ref = bf16[8,16,16,512]{3,2,1,0:T(8,128)(2,1)S(1)} async-done(((bf16[8,16,16,512]{3,2,1,0:T(8,128)(2,1)}), bf16[8,16,16,512]{3,2,1,0:T(8,128)(2,1)S(1)}, u32[]{:S(2)}, u32[]{:S(2)}) %all-to-all-start) | async-done | bytes 2097184 | tf_op jit(solution)/shard_map/all_to_all | solution.py:246
  65.7 3.6 all-to-all-start.1
  69.3 6.9 %shard_map.229 = bf16[8,16,16,512]{3,2,1,0:T(8,128)(2,1)} custom-call(bf16[16,256,512]{2,1,0:T(8,128)(2,1)} %bitcast.75, bf16[16,256,512]{2,1,0:T(8,128)(2,1)} %bitcast.72, f32[16,1,1]{2,1,0:T(1,128)} %reshape.396.ns_ref), custom_call_target="tpu_custom_call" | custom-call | flops 1000000000 | bytes 4194304 | tf_op jit(solution)/shard_map/pallas_call | solution.py:195
  76.3 42.0 %all-to-all-done.1.half_ref = bf16[8,32,16,256]{3,2,1,0:T(8,128)(2,1)S(1)} async-done(((bf16[8,32,16,256]{3,2,1,0:T(8,128)(2,1)}), bf16[8,32,16,256]{3,2,1,0:T(8,128)(2,1)S(1)}, u32[]{:S(2)}, u32[]{:S(2)}) %all-to-all-start.1) | async-done | bytes 2097184 | tf_op jit(solution)/shard_map/all_to_all | solution.py:246
  119.6 4.4 %all-to-all-start.2 = ((bf16[8,16,16,512]{3,2,1,0:T(8,128)(2,1)}), bf16[8,16,16,512]{3,2,1,0:T(8,128)(2,1)}, u32[]{:S(2)}, u32[]{:S(2)}) async-start(bf16[8,16,16,512]{3,2,1,0:T(8,128)(2,1)} %shard_map.229), calls=%async_computation.2 | async-start | bytes 4194304 | tf_op jit(solution)/shard_map/all_to_all | solution.py:246
  128.0 13.0 %shard_map.232 = bf16[8,16,16,512]{3,2,1,0:T(8,128)(2,1)} custom-call(bf16[8,32,16,256]{3,2,1,0:T(8,128)(2,1)} %copy-done.1, bf16[256,512]{1,0:T(8,128)(2,1)} %constant.140.clone.fth, bf16[256,512]{1,0:T(8,128)(2,1)} %constant.141.clone.ftl, bf16[384,128]{1,0:T(8,128)(2,1)} %bitcast.84, f32[384,1]{1,0:T(8,128)} %reshape.397.b_in, bf16[384,384]{1,0:T(8,128)(2,1)} %bitcast.79, ...), custom_call_target="tpu_custom_call" | custom-call | flops 10000000000 | bytes 4194304 | tf_op jit(solution)/shard_map/pallas_call | solution.py:195
  140.9 32.0 %all-to-all-done.2.grad_ref = bf16[8,16,16,512]{3,2,1,0:T(8,128)(2,1)} async-done(((bf16[8,16,16,512]{3,2,1,0:T(8,128)(2,1)}), bf16[8,16,16,512]{3,2,1,0:T(8,128)(2,1)}, u32[]{:S(2)}, u32[]{:S(2)}) %all-to-all-start.2) | async-done | bytes 2097184 | tf_op jit(solution)/shard_map/all_to_all | solution.py:246
  173.0 3.6 all-to-all-start.3
  178.4 28.2 %shard_map.230 = (bf16[8,32,16,256]{3,2,1,0:T(8,128)(2,1)}, f32[384,640]{1,0:T(8,128)}, f32[384,256]{1,0:T(8,128)}) custom-call(bf16[8,32,16,256]{3,2,1,0:T(8,128)(2,1)} %copy-done.1, bf16[8,16,16,512]{3,2,1,0:T(8,128)(2,1)} %copy-done.2, f32[384,640]{1,0:T(8,128)} %broadcast_in_dim.24.acc_in, f32[384,256]{1,0:T(8,128)} %broadcast_in_dim.25.bias_in, ...), custom_call_target="tpu_custom_call" | custom-call | flops 30000001024 | bytes 4194304 | tf_op jit(solution)/shard_map/pallas_call | solution.py:195
  206.6 28.3 %shard_map.231 = (bf16[8,32,16,256]{3,2,1,0:T(8,128)(2,1)}, f32[384,640]{1,0:T(8,128)}, f32[384,256]{1,0:T(8,128)}) custom-call(bf16[8,32,16,256]{3,2,1,0:T(8,128)(2,1)} %copy-done.1, bf16[8,16,16,512]{3,2,1,0:T(8,128)(2,1)} %all-to-all-done.2.grad_ref, f32[384,640]{1,0:T(8,128)} %get-tuple-element.28.acc_in, ...), custom_call_target="tpu_custom_call", output_to_operand_aliasing={{0}: (14, {})} | custom-call | flops 30000001024 | bytes 4194304 | tf_op jit(solution)/shard_map/pallas_call | solution.py:195
  236.3 5.0 %all-to-all-start.4 = ((bf16[8,32,16,256]{3,2,1,0:T(8,128)(2,1)}), bf16[8,32,16,256]{3,2,1,0:T(8,128)(2,1)S(1)}, u32[]{:S(2)}, u32[]{:S(2)}) async-start(bf16[8,32,16,256]{3,2,1,0:T(8,128)(2,1)} %get-tuple-element.33), calls=%async_computation.4 | async-start | bytes 4194304 | tf_op jit(solution)/shard_map/all_to_all | solution.py:246
  247.2 1.5 collective-permute-start
  249.7 1.6 collective-permute-start.1
  252.1 1.4 collective-permute-start.2
  253.5 4.6 %collective-permute-done = f32[8,12,642]{2,0,1:T(8,128)S(1)} collective-permute-done((f32[8,12,642]{2,0,1:T(8,128)S(1)}, f32[8,12,642]{2,0,1:T(8,128)S(1)}, u32[]{:S(2)}, u32[]{:S(2)}) %collective-permute-start) | collective-permute-done | bytes 246560 | tf_op jit(solution)/shard_map/ppermute | solution.py:352
  258.1 5.8 %collective-permute-done.1 = f32[8,12,642]{2,0,1:T(8,128)S(1)} collective-permute-done((f32[8,12,642]{2,0,1:T(8,128)}, f32[8,12,642]{2,0,1:T(8,128)S(1)}, u32[]{:S(2)}, u32[]{:S(2)}) %collective-permute-start.1) | collective-permute-done | bytes 246560 | tf_op jit(solution)/shard_map/ppermute | solution.py:352
  265.6 1.7 collective-permute-start.4
  267.3 2.3 collective-permute-start.5
  269.6 1.5 collective-permute-start.6
  272.1 8.6 %collective-permute-done.3 = f32[12,642]{1,0:T(8,128)S(1)} collective-permute-done((f32[12,642]{1,0:T(8,128)S(1)}, f32[12,642]{1,0:T(8,128)S(1)}, u32[]{:S(2)}, u32[]{:S(2)}) %collective-permute-start.3) | collective-permute-done | bytes 30848 | tf_op jit(solution)/shard_map/ppermute | solution.py:352
  281.8 13.0 %shard_map.228 = bf16[8,16,16,512]{3,2,1,0:T(8,128)(2,1)} custom-call(bf16[8,32,16,256]{3,2,1,0:T(8,128)(2,1)} %copy-done.1, bf16[256,512]{1,0:T(8,128)(2,1)} %constant.140.clone.fth, bf16[256,512]{1,0:T(8,128)(2,1)} %constant.141.clone.ftl, bf16[384,128]{1,0:T(8,128)(2,1)} %bitcast.87, f32[384,1]{1,0:T(8,128)} %reshape.397.b_in, bf16[384,384]{1,0:T(8,128)(2,1)} %bitcast.82, ...), custom_call_target="tpu_custom_call" | custom-call | flops 10000000000 | bytes 4194304 | tf_op jit(solution)/shard_map/pallas_call | solution.py:195
  296.3 16.0 %all-to-all-start.5 = ((bf16[8,16,16,512]{3,2,1,0:T(8,128)(2,1)}), bf16[8,16,16,512]{3,2,1,0:T(8,128)(2,1)}, u32[]{:S(2)}, u32[]{:S(2)}) async-start(bf16[8,16,16,512]{3,2,1,0:T(8,128)(2,1)} %shard_map.228), calls=%async_computation.5 | async-start | bytes 4194304 | tf_op jit(solution)/shard_map/all_to_all | solution.py:246
  312.3 14.3 %shard_map.235.g_ref = f32[16,128,256]{2,1,0:T(8,128)} custom-call(bf16[16,256,512]{2,1,0:T(8,128)(2,1)} %bitcast.73, bf16[512,256]{1,0:T(8,128)(2,1)} %constant.138.clone.fh, bf16[512,256]{1,0:T(8,128)(2,1)} %constant.139.clone.fl, bf16[128,256]{1,0:T(8,128)(2,1)} %constant.144.clone.ath, bf16[128,256]{1,0:T(8,128)(2,1)} %constant.145.clone.atl), custom_call_target="tpu_custom_call" | custom-call | flops 10000000000 | bytes 4194304 | tf_op jit(solution)/shard_map/pallas_call | solution.py:195
  328.4 8.1 %shard_map.233.rest_0_ = f32[16,256,512]{2,1,0:T(8,128)} custom-call(bf16[8,16,16,512]{3,2,1,0:T(8,128)(2,1)} %copy-done, f32[16,256,512]{2,1,0:T(8,128)} %get-tuple-element.37.dyn_ref, bf16[16,256,512]{2,1,0:T(8,128)(2,1)} %bitcast.76, f32[16,1,1]{2,1,0:T(1,128)} %reshape.396.ns_ref), custom_call_target="tpu_custom_call" | custom-call | flops 10000000000 | bytes 4194304 | tf_op jit(solution)/shard_map/pallas_call | solution.py:195
  336.5 2.1 copy.113
  338.6 18.6 %shard_map.236 = f32[16,256,512]{2,1,0:T(8,128)} custom-call(bf16[16,256,256]{2,1,0:T(8,128)(2,1)} %bitcast.78, f32[16,128,256]{2,1,0:T(8,128)} %shard_map.235.g_ref, f32[16,1,128]{2,1,0:T(1,128)} %get-tuple-element.79.c_ref, f32[16,1,128]{2,1,0:T(1,128)} %get-tuple-element.78.s_ref, f32[16,128,1]{2,1,0:T(8,128)} %exponential_multiply_fusion.d_ref, ...), custom_call_target="tpu_custom_call" | custom-call | flops 20000000000 | bytes 4194304 | tf_op jit(solution)/shard_map/pallas_call | solution.py:195
  357.3 4.2 %all-to-all-done.5.tend_ref = bf16[8,16,16,512]{3,2,1,0:T(8,128)(2,1)} async-done(((bf16[8,16,16,512]{3,2,1,0:T(8,128)(2,1)}), bf16[8,16,16,512]{3,2,1,0:T(8,128)(2,1)}, u32[]{:S(2)}, u32[]{:S(2)}) %all-to-all-start.5) | async-done | bytes 2097184 | tf_op jit(solution)/shard_map/all_to_all | solution.py:246
  361.4 8.1 %shard_map.234 = f32[16,256,512]{2,1,0:T(8,128)} custom-call(bf16[8,16,16,512]{3,2,1,0:T(8,128)(2,1)} %all-to-all-done.5.tend_ref, f32[16,256,512]{2,1,0:T(8,128)} %get-tuple-element.37.dyn_ref, bf16[16,256,512]{2,1,0:T(8,128)(2,1)} %bitcast.77, f32[16,1,1]{2,1,0:T(1,128)} %reshape.396.ns_ref, ...), custom_call_target="tpu_custom_call", output_to_operand_aliasing={{}: (4, {})} | custom-call | flops 10000000000 | bytes 4194304 | tf_op jit(solution)/shard_map/pallas_call | solution.py:195
  (72 shorter events, 28.4 us)
Async XLA Ops:
  8.9 6.5 %copy-start.9 = (f32[4,4]{1,0:T(4,128)S(1)}, f32[4,4]{1,0:T(4,128)}, u32[]{:S(2)}) copy-start(f32[4,4]{1,0:T(4,128)} %param.23) | copy-start | bytes 196
  8.9 6.6 %copy-start.8 = (f32[4,4]{1,0:T(4,128)S(1)}, f32[4,4]{1,0:T(4,128)}, u32[]{:S(2)}) copy-start(f32[4,4]{1,0:T(4,128)} %param.22) | copy-start | bytes 196
  8.9 55.5 %all-to-all-start = ((bf16[8,16,16,512]{3,2,1,0:T(8,128)(2,1)}), bf16[8,16,16,512]{3,2,1,0:T(8,128)(2,1)S(1)}, u32[]{:S(2)}, u32[]{:S(2)}) async-start(bf16[8,16,16,512]{3,2,1,0:T(8,128)(2,1)} %shard_map.226), calls=%async_computation | async-start | bytes 4194304 | tf_op jit(solution)/shard_map/all_to_all | solution.py:246
  64.4 1.3 copy-start.2
  65.7 52.6 %all-to-all-start.1 = ((bf16[8,32,16,256]{3,2,1,0:T(8,128)(2,1)}), bf16[8,32,16,256]{3,2,1,0:T(8,128)(2,1)S(1)}, u32[]{:S(2)}, u32[]{:S(2)}) async-start(bf16[8,32,16,256]{3,2,1,0:T(8,128)(2,1)} %bitcast.5), calls=%async_computation.1 | async-start | bytes 4194304 | tf_op jit(solution)/shard_map/all_to_all | solution.py:246
  76.3 47.7 %copy-start.3 = (bf16[384,384]{1,0:T(8,128)(2,1)S(1)}, bf16[384,384]{1,0:T(8,128)(2,1)}, u32[]{:S(2)}) copy-start(bf16[384,384]{1,0:T(8,128)(2,1)} %w_mid.3) | copy-start | bytes 884740
  76.3 48.6 %copy-start.6 = (f32[384]{0:T(512)S(1)}, f32[384]{0:T(512)}, u32[]{:S(2)}) copy-start(f32[384]{0:T(512)} %param.26) | copy-start | bytes 4612
  76.3 49.4 %copy-start.7 = (f32[384]{0:T(512)S(1)}, f32[384]{0:T(512)}, u32[]{:S(2)}) copy-start(f32[384]{0:T(512)} %param.28) | copy-start | bytes 4612
  76.3 50.2 %copy-start.4 = (bf16[128,384]{1,0:T(8,128)(2,1)S(1)}, bf16[128,384]{1,0:T(8,128)(2,1)}, u32[]{:S(2)}) copy-start(bf16[128,384]{1,0:T(8,128)(2,1)} %w_in.3) | copy-start | bytes 294916
  76.3 50.9 %copy-start.5 = (bf16[384,128]{1,0:T(8,128)(2,1)S(1)}, bf16[384,128]{1,0:T(8,128)(2,1)}, u32[]{:S(2)}) copy-start(bf16[384,128]{1,0:T(8,128)(2,1)} %w_out.3) | copy-start | bytes 294916
  118.3 1.3 copy-start.1
  119.6 53.4 %all-to-all-start.2 = ((bf16[8,16,16,512]{3,2,1,0:T(8,128)(2,1)}), bf16[8,16,16,512]{3,2,1,0:T(8,128)(2,1)}, u32[]{:S(2)}, u32[]{:S(2)}) async-start(bf16[8,16,16,512]{3,2,1,0:T(8,128)(2,1)} %shard_map.229), calls=%async_computation.2 | async-start | bytes 4194304 | tf_op jit(solution)/shard_map/all_to_all | solution.py:246
  173.0 62.0 %all-to-all-start.3 = ((bf16[8,16,16,512]{3,2,1,0:T(8,128)(2,1)}), bf16[8,16,16,512]{3,2,1,0:T(8,128)(2,1)S(1)}, u32[]{:S(2)}, u32[]{:S(2)}) async-start(bf16[8,16,16,512]{3,2,1,0:T(8,128)(2,1)} %shard_map.232), calls=%async_computation.3 | async-start | bytes 4194304 | tf_op jit(solution)/shard_map/all_to_all | solution.py:246
  235.0 1.3 copy-start
  236.3 60.0 %all-to-all-start.4 = ((bf16[8,32,16,256]{3,2,1,0:T(8,128)(2,1)}), bf16[8,32,16,256]{3,2,1,0:T(8,128)(2,1)S(1)}, u32[]{:S(2)}, u32[]{:S(2)}) async-start(bf16[8,32,16,256]{3,2,1,0:T(8,128)(2,1)} %get-tuple-element.33), calls=%async_computation.4 | async-start | bytes 4194304 | tf_op jit(solution)/shard_map/all_to_all | solution.py:246
  247.2 10.9 %collective-permute-start = (f32[8,12,642]{2,0,1:T(8,128)S(1)}, f32[8,12,642]{2,0,1:T(8,128)S(1)}, u32[]{:S(2)}, u32[]{:S(2)}) collective-permute-start(f32[8,12,642]{2,0,1:T(8,128)S(1)} %bitcast.83), channel_id=1, source_target_pairs={{0,1},{1,2},{2,3},{3,0},{4,5},{5,6},{6,7},{7,4},{8,9},{9,10},{10,1... | collective-permute-start | bytes 739592 | tf_op jit(solution)/shard_map/ppermute | solution.py:352
  249.7 14.3 %collective-permute-start.1 = (f32[8,12,642]{2,0,1:T(8,128)}, f32[8,12,642]{2,0,1:T(8,128)S(1)}, u32[]{:S(2)}, u32[]{:S(2)}) collective-permute-start(f32[8,12,642]{2,0,1:T(8,128)} %bitcast.62), channel_id=1, source_target_pairs={{0,2},{1,3},{2,0},{3,1},{4,6},{5,7},{6,4},{7,5},{8,10},{9,11},{10,... | collective-permute-start | bytes 739592 | tf_op jit(solution)/shard_map/ppermute | solution.py:352
  252.1 12.0 %collective-permute-start.2 = (f32[8,12,642]{2,0,1:T(8,128)}, f32[8,12,642]{2,0,1:T(8,128)}, u32[]{:S(2)}, u32[]{:S(2)}) collective-permute-start(f32[8,12,642]{2,0,1:T(8,128)} %bitcast.61), channel_id=1, source_target_pairs={{0,3},{1,0},{2,1},{3,2},{4,7},{5,4},{6,5},{7,6},{8,11},{9,8},{10,9... | collective-permute-start | bytes 739592 | tf_op jit(solution)/shard_map/ppermute | solution.py:352
  265.5 15.1 %collective-permute-start.3 = (f32[12,642]{1,0:T(8,128)S(1)}, f32[12,642]{1,0:T(8,128)S(1)}, u32[]{:S(2)}, u32[]{:S(2)}) collective-permute-start(f32[12,642]{1,0:T(8,128)S(1)} %bitcast.96), channel_id=1, source_target_pairs={{0,4},{4,8},{8,12},{12,16},{16,20},{20,24},{24,28},{28,0},{1,5},{5... | collective-permute-start | bytes 92456 | tf_op jit(solution)/shard_map/ppermute | solution.py:352
  265.6 16.2 %collective-permute-start.4 = (f32[12,642]{1,0:T(8,128)S(1)}, f32[12,642]{1,0:T(8,128)S(1)}, u32[]{:S(2)}, u32[]{:S(2)}) collective-permute-start(f32[12,642]{1,0:T(8,128)S(1)} %bitcast.95), channel_id=1, source_target_pairs={{0,8},{4,12},{8,16},{12,20},{16,24},{20,28},{24,0},{28,4},{1,9},{5... | collective-permute-start | bytes 92456 | tf_op jit(solution)/shard_map/ppermute | solution.py:352
  267.3 27.7 %collective-permute-start.5 = (f32[12,642]{1,0:T(8,128)S(1)}, f32[12,642]{1,0:T(8,128)S(1)}, u32[]{:S(2)}, u32[]{:S(2)}) collective-permute-start(f32[12,642]{1,0:T(8,128)S(1)} %bitcast.90), channel_id=1, source_target_pairs={{0,12},{4,16},{8,20},{12,24},{16,28},{20,0},{24,4},{28,8},{1,13},{... | collective-permute-start | bytes 92456 | tf_op jit(solution)/shard_map/ppermute | solution.py:352
  269.6 26.6 %collective-permute-start.6 = (f32[12,642]{1,0:T(8,128)S(1)}, f32[12,642]{1,0:T(8,128)S(1)}, u32[]{:S(2)}, u32[]{:S(2)}) collective-permute-start(f32[12,642]{1,0:T(8,128)S(1)} %bitcast.91), channel_id=1, source_target_pairs={{0,16},{4,20},{8,24},{12,28},{16,0},{20,4},{24,8},{28,12},{1,17},{... | collective-permute-start | bytes 92456 | tf_op jit(solution)/shard_map/ppermute | solution.py:352
  271.1 25.2 %collective-permute-start.7 = (f32[12,642]{1,0:T(8,128)S(1)}, f32[12,642]{1,0:T(8,128)S(1)}, u32[]{:S(2)}, u32[]{:S(2)}) collective-permute-start(f32[12,642]{1,0:T(8,128)S(1)} %bitcast.92), channel_id=1, source_target_pairs={{0,20},{4,24},{8,28},{12,0},{16,4},{20,8},{24,12},{28,16},{1,21},{... | collective-permute-start | bytes 92456 | tf_op jit(solution)/shard_map/ppermute | solution.py:352
  280.6 15.6 %collective-permute-start.8 = (f32[12,642]{1,0:T(8,128)S(1)}, f32[12,642]{1,0:T(8,128)S(1)}, u32[]{:S(2)}, u32[]{:S(2)}) collective-permute-start(f32[12,642]{1,0:T(8,128)S(1)} %bitcast.94), channel_id=1, source_target_pairs={{0,24},{4,28},{8,0},{12,4},{16,8},{20,12},{24,16},{28,20},{1,25},{... | collective-permute-start | bytes 92456 | tf_op jit(solution)/shard_map/ppermute | solution.py:352
  281.8 14.5 %collective-permute-start.9 = (f32[12,642]{1,0:T(8,128)S(1)}, f32[12,642]{1,0:T(8,128)S(1)}, u32[]{:S(2)}, u32[]{:S(2)}) collective-permute-start(f32[12,642]{1,0:T(8,128)S(1)} %bitcast.93), channel_id=1, source_target_pairs={{0,28},{4,0},{8,4},{12,8},{16,12},{20,16},{24,20},{28,24},{1,29},{... | collective-permute-start | bytes 92456 | tf_op jit(solution)/shard_map/ppermute | solution.py:352
  296.3 65.1 %all-to-all-start.5 = ((bf16[8,16,16,512]{3,2,1,0:T(8,128)(2,1)}), bf16[8,16,16,512]{3,2,1,0:T(8,128)(2,1)}, u32[]{:S(2)}, u32[]{:S(2)}) async-start(bf16[8,16,16,512]{3,2,1,0:T(8,128)(2,1)} %shard_map.228), calls=%async_computation.5 | async-start | bytes 4194304 | tf_op jit(solution)/shard_map/all_to_all | solution.py:246
where the time goes:
time: 372 us; the launch traced here: 370 us
  Pallas kernels  173 us (47%)
  waiting for transfers between devices  115 us (31%)
  starting transfers between devices  50 us (13%)
  local copies, waits for them, and re-layouts  24.9 us (7%)
  other arithmetic  5.85 us (2%)
    pallas_call x11, Pallas kernels, call(): pl.pallas_call(kernel, grid=grid, in_specs=in_specs, out_specs=out_specs,...  173 us
    all_to_all x6, waiting for transfers between devices, exchange(): return lax.all_to_all(x, axis, split_axis=0, concat_axis=0, tiled=True)  93.6 us
    all_to_all x6, starting transfers between devices, exchange(): return lax.all_to_all(x, axis, split_axis=0, concat_axis=0, tiled=True)  39.1 us
    ppermute x10, waiting for transfers between devices, reduce_axis(): lax.ppermute(block, axis, [(s, (s + hop) % size) for s in range(size)])  21.7 us
    ppermute x10, starting transfers between devices, reduce_axis(): lax.ppermute(block, axis, [(s, (s + hop) % size) for s in range(size)])  11 us
  transfers between devices with their start and end apart: 16, of which 11 were waited for; matrix products, arithmetic and copies ran while one was open for 7% of the time, Pallas kernels for 43%

commit v1 on v0

v1 whole, which is shorter than its diff:
```python
import math

import jax
import jax.numpy as jnp
import numpy as np
from jax import lax
from jax.experimental import pallas as pl
from jax.experimental.pallas import tpu as pltpu
from jax.sharding import PartitionSpec as P


WAVES = 128
MODES = 128
BF = jnp.bfloat16
F32 = jnp.float32


def dot(a, b):
    return lax.dot_general(a, b, (((1,), (0,)), ((), ())), preferred_element_type=F32)


def dot_t(a, b):
    return lax.dot_general(a, b, (((1,), (1,)), ((), ())), preferred_element_type=F32)


def split(x):
    hi = x.astype(BF)
    return hi, (x - hi.astype(F32)).astype(BF)


def dot3(a, b):
    return dot(a[0], b[0]) + (dot(a[1], b[0]) + dot(a[0], b[1]))


def host_split(table):
    table = table.astype(np.float32)
    hi = table.astype(BF)
    lo = (table - hi.astype(np.float32)).astype(BF)
    return np.ascontiguousarray(hi), np.ascontiguousarray(lo)


def spectral_tables(lat_count, lon_count):
    turn = (np.arange(lon_count)[:, None] * np.arange(WAVES)[None, :]) % lon_count
    angle = 2.0 * np.pi * turn / lon_count
    lon = np.concatenate([np.cos(angle), np.sin(angle)], axis=1)
    lat = np.cos(np.pi * (np.arange(lat_count)[:, None] + 0.5) * np.arange(MODES)[None, :] / lat_count)
    return lon, lat


def rotation_rows(zonal_shift, viscosity, lat_count, lon_count):
    shift = zonal_shift.reshape(-1, 1, 1)
    visc = viscosity.reshape(-1, 1, 1)
    wave = jnp.arange(WAVES, dtype=F32)
    mode = jnp.arange(MODES, dtype=F32)
    wave_scale = jnp.where(wave == 0, 1.0, 2.0) / lon_count
    mode_scale = jnp.where(mode == 0, 1.0, 2.0) / lat_count
    damp_k = (jnp.exp(-visc * ((wave / WAVES) ** 2)[None, None, :]) * wave_scale)
    cosine = jnp.cos(shift * wave[None, None, :]) * damp_k
    sine = jnp.sin(shift * wave[None, None, :]) * damp_k
    damp_p = jnp.exp(-visc * ((mode / MODES) ** 2)[None, :, None]) * mode_scale[None, :, None]
    return cosine, sine, damp_p


def rotate(spec, cos_ref, sin_ref, damp_ref, sign):
    cosine = cos_ref[0]
    sine = sin_ref[0] * sign
    a = spec[:, :WAVES] * damp_ref[0]
    b = spec[:, WAVES:] * damp_ref[0]
    return jnp.concatenate([a * cosine - b * sine, a * sine + b * cosine], axis=1)


def pair(h_ref, l_ref):
    return h_ref[...], l_ref[...]


def swap_rows(x):
    return jnp.swapaxes(x.astype(F32), 0, 1)


def spectral_fwd_kernel(
    at_ref, x_ref, c_ref, s_ref, d_ref, fh, fl, fth, ftl, ah, al, ath, atl, dyn_ref, *rest
):
    outs, keep = rest[:-1], rest[-1]
    groups = len(outs)
    own = keep.shape[2]
    z = dot3(split(x_ref[0]), pair(fh, fl))
    spec = dot3(pair(ath, atl), split(z))
    rot = rotate(spec, c_ref, s_ref, d_ref, 1.0)
    half = split(dot3(pair(ah, al), split(rot)))
    dyn_ref[0] = dot3(half, pair(fth, ftl))
    step = pl.program_id(0)
    for g in range(groups):
        keep[step, g] = half[0][g * own : (g + 1) * own]

    @pl.when(step == pl.num_programs(0) - 1)
    def _():
        for hop in range(groups):
            dest = lax.rem(at_ref[0] + hop, groups)
            outs[hop][...] = swap_rows(keep[:, dest]).astype(BF)


def cot_spec_kernel(x_ref, fh, fl, ath, atl, out_ref):
    x = x_ref[0]
    z = dot(x, fh[...]) + dot(x, fl[...])
    out_ref[0] = dot3(pair(ath, atl), split(z))


def spectral_bwd_kernel(g_ref, c_ref, s_ref, d_ref, fth, ftl, ah, al, ath, atl, *rest):
    backs, out_ref, keep = rest[:-2], rest[-2], rest[-1]
    own = backs[0].shape[0]
    step = pl.program_id(0)

    @pl.when(step == 0)
    def _():
        for hop, ref in enumerate(backs):
            keep[:, hop * own : (hop + 1) * own, :] = swap_rows(ref[...]).astype(BF)

    b = keep[step]
    spec = dot(ath[...], b) + dot(atl[...], b) + g_ref[0]
    rot = rotate(spec, c_ref, s_ref, d_ref, -1.0)
    half = split(dot3(pair(ah, al), split(rot)))
    out_ref[0] = dot3(half, pair(fth, ftl))


def grad_tend_kernel(at_ref, noise_ref, cot_ref, ns_ref, *outs):
    groups = len(outs)
    for hop in range(groups):
        dest = lax.rem(at_ref[0] + hop, groups)
        factor = 1.0 + ns_ref[...] * noise_ref[:, dest].astype(F32)
        outs[hop][...] = swap_rows(cot_ref[:, dest].astype(F32) * factor).astype(BF)


def next_state_kernel(at_ref, dyn_ref, noise_ref, ns_ref, *rest):
    groups = dyn_ref.shape[1]
    tends, out_ref = rest[:groups], rest[-1]
    for hop in range(groups):
        src = lax.rem(at_ref[0] + (groups - hop), groups)
        factor = 1.0 + ns_ref[...] * noise_ref[:, src].astype(F32)
        out_ref[:, src] = dyn_ref[:, src] + swap_rows(tends[hop][...]) * factor


def sigmoid(x):
    return 0.5 * jnp.tanh(0.5 * x) + 0.5


def rows_of(refs, row):
    return jnp.concatenate([ref[row] for ref in refs], axis=0)


def inputs_of(halves, fth, ftl, rows):
    parts = []
    for row in range(rows):
        h = rows_of(halves, row)
        parts.append((dot(h, fth[...]) + dot(h, ftl[...])).astype(BF))
    return jnp.concatenate(parts, axis=1)


def columns_fwd_kernel(fth, ftl, w_in_t, b_in, w_mid_t, b_mid, w_out_t, *rest):
    groups = len(rest) // 2
    halves, outs = rest[:groups], rest[groups:]
    rows, per_group, lon_count = outs[0].shape
    inputs = inputs_of(halves, fth, ftl, rows)
    pre_one = dot(w_in_t[...], inputs) + b_in[...]
    act_one = (pre_one * sigmoid(pre_one)).astype(BF)
    pre_two = dot(w_mid_t[...], act_one) + b_mid[...]
    act_two = (pre_two * sigmoid(pre_two)).astype(BF)
    tend = dot(w_out_t[...], act_two).astype(BF)
    for hop, ref in enumerate(outs):
        for row in range(rows):
            ref[row] = tend[hop * per_group : (hop + 1) * per_group, row * lon_count : (row + 1) * lon_count]


def lane_sums(x):
    total = x[:, :128]
    for at in range(128, x.shape[1], 128):
        total = total + x[:, at : at + 128]
    return total


def columns_bwd_kernel(
    acc_in, bias_in, fth, ftl, fh, w_in_t, b_in, w_mid_t, b_mid, w_in, w_mid, w_out, groups, *rest
):
    halves, grads = rest[:groups], rest[groups : 2 * groups]
    backs = rest[-groups - 2 : -2]
    acc_ref, bias_ref = rest[-2:]
    rows, per_group, lon_count = grads[0].shape
    ein = w_in.shape[0]
    hid = w_mid.shape[0]

    @pl.when(pl.program_id(0) == 0)
    def _():
        acc_ref[...] = acc_in[...]
        bias_ref[...] = bias_in[...]

    inputs = inputs_of(halves, fth, ftl, rows)
    grad = jnp.concatenate([rows_of(grads, row) for row in range(rows)], axis=1)
    pre_one = dot(w_in_t[...], inputs) + b_in[...]
    sig_one = sigmoid(pre_one)
    full_one = pre_one * sig_one
    act_one = full_one.astype(BF)
    silu_one = sig_one + full_one * (1.0 - sig_one)
    pre_two = dot(w_mid_t[...], act_one) + b_mid[...]
    sig_two = sigmoid(pre_two)
    full_two = pre_two * sig_two
    act_two = full_two.astype(BF)
    slope_two_f = dot(w_out[...], grad) * (sig_two + full_two * (1.0 - sig_two))
    slope_two = slope_two_f.astype(BF)
    slope_one_f = dot(w_mid[...], slope_two) * silu_one
    slope_one = slope_one_f.astype(BF)
    bias_ref[:, :128] += lane_sums(slope_one_f)
    bias_ref[:, 128:] += lane_sums(slope_two_f)
    acc_ref[:, :ein] += dot_t(slope_one, inputs)
    acc_ref[:, ein : ein + hid] += dot_t(slope_two, act_one)
    acc_ref[:, ein + hid :] += dot_t(act_two, grad)
    back = dot(w_in[...], slope_one).astype(BF)
    for row in range(rows):
        part = back[:, row * lon_count : (row + 1) * lon_count]
        out = dot(part, fh[...]).astype(BF)
        for hop, ref in enumerate(backs):
            ref[row] = out[hop * per_group : (hop + 1) * per_group]


def whole_spec(shape):
    return pl.BlockSpec(shape, lambda *_: (0,) * len(shape))


def call(kernel, grid, in_specs, out_specs, out_shape, flops, args, aliases=None, prefetch=0, scratch=()):
    return pl.pallas_call(
        kernel,
        grid_spec=pltpu.PrefetchScalarGridSpec(
            num_scalar_prefetch=prefetch,
            grid=grid,
            in_specs=in_specs,
            out_specs=out_specs,
            scratch_shapes=list(scratch),
        ),
        out_shape=out_shape,
        input_output_aliases=aliases or {},
        cost_estimate=pl.CostEstimate(flops=flops, transcendentals=0, bytes_accessed=1 << 22),
        compiler_params=pltpu.CompilerParams(
            dimension_semantics=("arbitrary",) * len(grid), vmem_limit_bytes=56 << 20
        ),
    )(*args)


def per_device(
    model_state, noise_field, cotangent, zonal_shift, viscosity, noise_scale, w_in, b_in, w_mid, b_mid, w_out
):
    members_here, levels, fields, nlat, nlon = model_state.shape
    groups = lax.axis_size("level")
    members = lax.axis_size("member")
    lf = levels * fields
    own = nlat // groups
    part = own // 2
    ein, hid = w_in.shape
    state = model_state.reshape(lf, nlat, nlon)
    noise = noise_field.reshape(lf, nlat, nlon)
    cot = cotangent.reshape(lf, nlat, nlon)
    scale = noise_scale.reshape(lf, 1, 1)
    lon, lat = spectral_tables(nlat, nlon)
    fh, fl = host_split(lon)
    ah, al = host_split(lat)
    ath, atl = host_split(lat.T)
    waves2 = fh.shape[1]

    def sds(shape, dtype):
        return jax.ShapeDtypeStruct(shape, dtype)

    at = lax.axis_index("level").astype(jnp.int32)
    at_one = at.reshape(1)
    chunk = 8

    def send_order(x):
        blocks = x.reshape((groups, -1) + x.shape[1:])
        blocks = jnp.concatenate([blocks, blocks], axis=0)
        return lax.dynamic_slice_in_dim(blocks, at, groups, 0).reshape(x.shape)

    def recv_order(x):
        blocks = x.reshape((groups, -1) + x.shape[1:])
        blocks = jnp.concatenate([blocks[:1], blocks[:0:-1]], axis=0)
        blocks = jnp.concatenate([blocks, blocks], axis=0)
        return lax.dynamic_slice_in_dim(blocks, (groups - at) % groups, groups, 0).reshape(x.shape)

    def rows_block(which):
        return pl.BlockSpec((lf, groups, chunk, nlon), lambda s, _: (0, 0, s + which * (part // chunk), 0))

    by_group = (lf, groups, own, nlon)

    def grad_part(which, *after):
        noise_here, cot_here = noise, cot
        if after:
            noise_here, cot_here = lax.optimization_barrier((noise, cot) + after)[:2]
        return call(
            grad_tend_kernel,
            (part // chunk,),
            [rows_block(which), rows_block(which), whole_spec((lf, 1, 1))],
            [pl.BlockSpec((chunk, lf, nlon), lambda s, _: (s, 0, 0))] * groups,
            [sds((part, lf, nlon), BF)] * groups,
            10**9,
            (at_one, noise_here.reshape(by_group), cot_here.reshape(by_group), scale),
            prefetch=1,
        )

    def exchange(blocks):
        got = [blocks[0]]
        for hop in range(1, groups):
            got.append(lax.ppermute(blocks[hop], "level", [(s, (s + hop) % groups) for s in range(groups)]))
        return got

    per_lf = lambda *shape: pl.BlockSpec((1,) + shape, lambda s, *_: (s,) + (0,) * len(shape))
    row_spec = per_lf(1, WAVES)
    col_spec = per_lf(MODES, 1)
    f_specs = [whole_spec(fh.shape)] * 2
    ft_specs = [whole_spec(fh.shape[::-1])] * 2
    a_specs = [whole_spec(ah.shape)] * 2
    at_specs = [whole_spec(ath.shape)] * 2

    sends = grad_part(0)
    grad_one = exchange(sends)
    state, shift, visc, w_in, w_mid, w_out, at, fh, fl, _ = lax.optimization_barrier(
        (state, zonal_shift, viscosity, w_in, w_mid, w_out, at, jnp.asarray(fh), jnp.asarray(fl), sends[0])
    )
    fth, ftl = fh.T, fl.T
    cosine, sine, damp_p = rotation_rows(shift, visc, nlat, nlon)
    dyn, *sends = call(
        spectral_fwd_kernel,
        (lf,),
        [per_lf(nlat, nlon), row_spec, row_spec, col_spec] + f_specs + ft_specs + a_specs + at_specs,
        [per_lf(nlat, nlon)] + [whole_spec((own, lf, waves2))] * groups,
        [sds((lf, nlat, nlon), F32)] + [sds((own, lf, waves2), BF)] * groups,
        2 * 10**10,
        (at_one, state, cosine, sine, damp_p, fh, fl, fth, ftl, ah, al, ath, atl),
        prefetch=1,
        scratch=[pltpu.VMEM((lf, groups, own, waves2), BF)],
    )
    cols = exchange(sends)
    sends = grad_part(1, sends[0])
    held = lax.optimization_barrier((*sends, *cols))
    cols = held[groups:]
    grad_two = exchange(held[:groups])
    cot_spec = call(
        cot_spec_kernel,
        (lf,),
        [per_lf(nlat, nlon)] + f_specs + at_specs,
        per_lf(MODES, waves2),
        sds((lf, MODES, waves2), F32),
        10**10,
        (cot, fh, fl, ath, atl),
    )

    w_in_t = recv_order(w_in).T
    w_in_send = send_order(w_in)
    w_mid_t = w_mid.T
    w_out_t = w_out.T
    w_out_recv = recv_order(w_out_t).T
    w_out_t = send_order(w_out_t)
    bias_one = b_in.reshape(hid, 1)
    bias_two = b_mid.reshape(hid, 1)
    step = 2
    steps = part // step

    def half_spec(which):
        return pl.BlockSpec((step, lf, waves2), lambda s: (s + which * steps, 0, 0))

    grid_spec = pl.BlockSpec((step, lf, nlon), lambda s: (s, 0, 0))

    def forward(which):
        return call(
            columns_fwd_kernel,
            (steps,),
            ft_specs
            + [whole_spec(v.shape) for v in (w_in_t, bias_one, w_mid_t, bias_two, w_out_t)]
            + [half_spec(which)] * groups,
            [grid_spec] * groups,
            [sds((part, lf, nlon), BF)] * groups,
            10**10,
            (fth, ftl, w_in_t, bias_one, w_mid_t, bias_two, w_out_t, *cols),
        )

    acc_shape = (hid, 2 * ein + hid)
    sums_shape = (hid, 256)

    def backward(which, grads, acc, sums, before):
        args = (acc, sums, fth, ftl, fh, w_in_t, bias_one, w_mid_t, bias_two, w_in_send, w_mid, w_out_recv)
        specs = [whole_spec(v.shape) for v in args]
        args = args + (*cols, *grads)
        specs = specs + [half_spec(which)] * groups + [grid_spec] * groups
        aliases = {}
        if before is not None:
            aliases = {len(args) + hop: hop for hop in range(groups)}
            specs = specs + [pl.BlockSpec(memory_space=pl.ANY)] * groups
            args = args + tuple(before)
        *back, acc, sums = call(
            lambda *refs: columns_bwd_kernel(*refs[:12], groups, *refs[12:]),
            (steps,),
            specs,
            [half_spec(which)] * groups + [whole_spec(acc_shape), whole_spec(sums_shape)],
            [sds((own, lf, waves2), BF)] * groups + [sds(acc_shape, F32), sds(sums_shape, F32)],
            3 * 10**10,
            args,
            aliases,
        )
        return back, acc, sums

    sends_one = forward(0)
    back, acc, sums = backward(0, grad_one, jnp.zeros(acc_shape, F32), jnp.zeros(sums_shape, F32), None)
    *sends_one, sums = lax.optimization_barrier((*sends_one, sums))
    tend_one = exchange(sends_one)
    back, acc, sums = backward(1, grad_two, acc, sums, back)
    back = exchange(back)
    acc, *cols = lax.optimization_barrier((acc, *cols))
    sends_two = forward(1)

    def reduce_axis(x, axis):
        size = lax.axis_size(axis)
        at = lax.axis_index(axis)
        total = lax.dynamic_index_in_dim(x, at, 0, keepdims=False)
        for hop in range(1, size):
            block = lax.dynamic_index_in_dim(x, (at + hop) % size, 0, keepdims=False)
            total = total + lax.ppermute(block, axis, [(s, (s + hop) % size) for s in range(size)])
        return total

    sums_two = jnp.stack([jnp.sum(sums[:, :128], axis=1), jnp.sum(sums[:, 128:], axis=1)], axis=1)
    index = jnp.arange(ein)
    source = (at + groups - index // lf) % groups * lf + index % lf
    place = (source[:, None] == index[None, :]).astype(F32)
    sorted_in = jnp.dot(acc[:, :ein], place, precision=lax.Precision.HIGHEST)
    sorted_out = jnp.dot(acc[:, ein + hid :], place, precision=lax.Precision.HIGHEST)
    packed = jnp.concatenate([sorted_in, acc[:, ein : ein + hid], sorted_out, sums_two], axis=1)
    width = packed.shape[1]
    share = hid // (groups * members)
    packed = packed.reshape(groups, members, share, width).transpose(1, 0, 2, 3)
    packed = reduce_axis(packed, "member")
    packed = reduce_axis(packed, "level")
    packed = packed * (1.0 / math.sqrt(members_here * members * nlat * nlon))
    packed = packed.T
    tend_two = exchange(sends_two)

    def finish(which, tend, before):
        rows = rows_block(which)
        specs = [rows, rows, whole_spec((lf, 1, 1))]
        specs = specs + [pl.BlockSpec((chunk, lf, nlon), lambda s, _: (s, 0, 0))] * groups
        args = (at_one, dyn.reshape(by_group), noise.reshape(by_group), scale, *tend)
        aliases = {}
        if before is not None:
            aliases = {len(args): 0}
            specs = specs + [pl.BlockSpec(memory_space=pl.ANY)]
            args = args + (before,)
        return call(
            next_state_kernel, (part // chunk,), specs, rows, sds(by_group, F32), 10**10, args, aliases, prefetch=1
        )

    next_state = finish(0, tend_one, None)
    lat_recv = recv_order(jnp.concatenate([jnp.asarray(ah), jnp.asarray(al)], axis=1)).T
    state_grad = call(
        spectral_bwd_kernel,
        (lf,),
        [per_lf(MODES, waves2), row_spec, row_spec, col_spec]
        + ft_specs
        + a_specs
        + at_specs
        + [whole_spec((own, lf, waves2))] * groups,
        per_lf(nlat, nlon),
        sds((lf, nlat, nlon), F32),
        2 * 10**10,
        (cot_spec, cosine, sine, damp_p, fth, ftl, ah, al, lat_recv[:MODES], lat_recv[MODES:], *back),
        scratch=[pltpu.VMEM((lf, nlat, waves2), BF)],
    )
    next_state = finish(1, tend_two, next_state)

    shape = model_state.shape
    return (
        next_state.reshape(shape),
        state_grad.reshape(shape),
        packed[:ein],
        packed[ein : ein + hid],
        packed[ein + hid : 2 * ein + hid],
        packed[2 * ein + hid :],
    )


def solution(mesh):
    big = P("member", "level", None, None, None)
    small = P("level", None)
    grads = P(None, ("level", "member"))
    return jax.shard_map(
        per_device,
        mesh=mesh,
        in_specs=(big, big, big, small, small, small, P(), P(), P(), P(), P()),
        out_specs=(big, big, grads, grads, grads, grads),
        check_vma=False,
    )
```

time: 372 us -> 380 us (1.022)
  starting transfers between devices: 50 us -> 125 us
  waiting for transfers between devices: 115 us -> 64.6 us
  local copies, waits for them, and re-layouts: 24.9 us -> 16 us
  Pallas kernels: 173 us -> 167 us
    ppermute x0 -> x42, starting transfers between devices: none -> 114 us  [exchange(): lax.ppermute(blocks[hop], 'level', [(s, (s + hop) % groups) for s in rang...]
    all_to_all x6 -> x0, waiting for transfers between devices: 93.6 us -> none  [exchange(): return lax.all_to_all(x, axis, split_axis=0, concat_axis=0, tiled=True)]
    ppermute x0 -> x42, waiting for transfers between devices: none -> 56.6 us  [exchange(): lax.ppermute(blocks[hop], 'level', [(s, (s + hop) % groups) for s in rang...]
    all_to_all x6 -> x0, starting transfers between devices: 39.1 us -> none  [exchange(): return lax.all_to_all(x, axis, split_axis=0, concat_axis=0, tiled=True)]
    ppermute x10, waiting for transfers between devices: 21.7 us -> 7.97 us  [reduce_axis(): lax.ppermute(block, axis, [(s, (s + hop) % size) for s in range(size)])]
    pallas_call x11, Pallas kernels: 173 us -> 167 us  [call(): pl.pallas_call(kernel, grid_spec=pltpu.PrefetchScalarGridSpec(num_scalar_...]
    unnamed x31 -> x114, local copies, waits for them, and re-layouts: 7.04 us -> 1.94 us
    pallas_call x1 -> x0, local copies, waits for them, and re-layouts: 4.08 us -> none  [call(): pl.pallas_call(kernel, grid=grid, in_specs=in_specs, out_specs=out_specs,...]
  transfers between devices with their start and end apart: 16 -> 52, of which waited for: 11 -> 11; matrix products, arithmetic and copies ran while one was open for 7% -> 3% of each run, Pallas kernels for 43% -> 35%
where the time goes in v1:
time: 380 us; the launch traced here: 379 us
  Pallas kernels  167 us (44%)
  starting transfers between devices  125 us (33%)
  waiting for transfers between devices  64.6 us (17%)
  local copies, waits for them, and re-layouts  16 us (4%)
  other arithmetic  4.21 us (1%)
    pallas_call x11, Pallas kernels, call(): pl.pallas_call(kernel, grid_spec=pltpu.PrefetchScalarGridSpec(num_scalar_...  167 us
    ppermute x42, starting transfers between devices, exchange(): lax.ppermute(blocks[hop], 'level', [(s, (s + hop) % groups) for s in rang...  114 us
    ppermute x42, waiting for transfers between devices, exchange(): lax.ppermute(blocks[hop], 'level', [(s, (s + hop) % groups) for s in rang...  56.6 us
    ppermute x10, starting transfers between devices, reduce_axis(): lax.ppermute(block, axis, [(s, (s + hop) % size) for s in range(size)])  11.3 us
    ppermute x10, waiting for transfers between devices, reduce_axis(): lax.ppermute(block, axis, [(s, (s + hop) % size) for s in range(size)])  7.97 us
  transfers between devices with their start and end apart: 52, of which 11 were waited for; matrix products, arithmetic and copies ran while one was open for 3% of the time, Pallas kernels for 35%

profile of v1, /device:TPU:0, one launch (start us, length us, event | category | flops | bytes accessed | tf_op | source)
XLA Modules:
  0.0 379.3 jit_solution(10703053035944797894)
XLA Ops:
  2.1 4.2 %shard_map.208 = (bf16[16,16,512]{2,1,0:T(8,128)(2,1)}, bf16[16,16,512]{2,1,0:T(8,128)(2,1)}, bf16[16,16,512]{2,1,0:T(8,128)(2,1)}, bf16[16,16,512]{2,1,0:T(8,12...) custom-call(s32[1]{0:T(128)} %bitcast.at_ref, ...), custom_call_target="tpu_custom_call" | custom-call | flops 1000000000 | bytes 4194304 | tf_op jit(solution)/shard_map/pallas_call | solution.py:228
  10.5 29.0 %shard_map.209 = (f32[16,256,512]{2,1,0:T(8,128)}, bf16[32,16,256]{2,1,0:T(8,128)(2,1)}, bf16[32,16,256]{2,1,0:T(8,128)(2,1)}, bf16[32,16,256]{2,1,0:T(8,128)(2,...) custom-call(s32[1]{0:T(128)} %bitcast.at_ref, ...), custom_call_target="tpu_custom_call" | custom-call | flops 20000000000 | bytes 4194304 | tf_op jit(solution)/shard_map/pallas_call | solution.py:228
  40.0 2.6 collective-permute-start.1
  42.6 2.5 collective-permute-start.2
  47.6 14.4 %shard_map.217.g_ref = f32[16,128,256]{2,1,0:T(8,128)} custom-call(bf16[16,256,512]{2,1,0:T(8,128)(2,1)} %bitcast.90, bf16[512,256]{1,0:T(8,128)(2,1)} %copy.118.fh.refs_4_, bf16[512,256]{1,0:T(8,128)(2,1)} %copy.119.fl, bf16[128,256]{1,0:T(8,128)(2,1)} %constant.181.clone.ath, bf16[128,256]{1,0:T(8,128)(2,1)} %constant.182.clone.atl), custom_call_target="tpu_custom_call" | custom-call | flops 10000000000 | bytes 4194304 | tf_op jit(solution)/shard_map/pallas_call | solution.py:228
  64.9 8.7 %collective-permute-done.2.refs_15_.rest_3_ = bf16[32,16,256]{2,1,0:T(8,128)(2,1)S(1)} collective-permute-done((bf16[32,16,256]{2,1,0:T(8,128)(2,1)}, bf16[32,16,256]{2,1,0:T(8,128)(2,1)S(1)}, u32[]{:S(2)}, u32[]{:S(2)}) %collective-permute-start.2) | collective-permute-done | bytes 262176 | tf_op jit(solution)/shard_map/ppermute | solution.py:307
  73.8 11.1 %collective-permute-start.8 = (bf16[16,16,512]{2,1,0:T(8,128)(2,1)}, bf16[16,16,512]{2,1,0:T(8,128)(2,1)}, u32[]{:S(2)}, u32[]{:S(2)}) collective-permute-start(bf16[16,16,512]{2,1,0:T(8,128)(2,1)} %get-tuple-element.150), channel_id=1, source_target_pairs={{0,8},{4,12},{8,16},{12,20},{16,24},{20,28},{24,0},{28,4},{1,9},{5... | collective-permute-start | bytes 786440 | tf_op jit(solution)/shard_map/ppermute | solution.py:307
  85.2 4.2 %collective-permute-start.9 = (bf16[16,16,512]{2,1,0:T(8,128)(2,1)}, bf16[16,16,512]{2,1,0:T(8,128)(2,1)}, u32[]{:S(2)}, u32[]{:S(2)}) collective-permute-start(bf16[16,16,512]{2,1,0:T(8,128)(2,1)} %get-tuple-element.151), channel_id=1, source_target_pairs={{0,12},{4,16},{8,20},{12,24},{16,28},{20,0},{24,4},{28,8},{1,13},{... | collective-permute-start | bytes 786440 | tf_op jit(solution)/shard_map/ppermute | solution.py:307
  89.4 3.9 %collective-permute-start.10 = (bf16[16,16,512]{2,1,0:T(8,128)(2,1)}, bf16[16,16,512]{2,1,0:T(8,128)(2,1)}, u32[]{:S(2)}, u32[]{:S(2)}) collective-permute-start(bf16[16,16,512]{2,1,0:T(8,128)(2,1)} %get-tuple-element.152), channel_id=1, source_target_pairs={{0,16},{4,20},{8,24},{12,28},{16,0},{20,4},{24,8},{28,12},{1,17},{... | collective-permute-start | bytes 786440 | tf_op jit(solution)/shard_map/ppermute | solution.py:307
  93.3 13.4 %collective-permute-start.11 = (bf16[16,16,512]{2,1,0:T(8,128)(2,1)}, bf16[16,16,512]{2,1,0:T(8,128)(2,1)}, u32[]{:S(2)}, u32[]{:S(2)}) collective-permute-start(bf16[16,16,512]{2,1,0:T(8,128)(2,1)} %get-tuple-element.153), channel_id=1, source_target_pairs={{0,20},{4,24},{8,28},{12,0},{16,4},{20,8},{24,12},{28,16},{1,21},{... | collective-permute-start | bytes 786440 | tf_op jit(solution)/shard_map/ppermute | solution.py:307
  106.7 3.1 collective-permute-start.12
  109.8 4.0 %shard_map.210 = (bf16[16,16,512]{2,1,0:T(8,128)(2,1)}, bf16[16,16,512]{2,1,0:T(8,128)(2,1)}, bf16[16,16,512]{2,1,0:T(8,128)(2,1)}, bf16[16,16,512]{2,1,0:T(8,12...) custom-call(s32[1]{0:T(128)} %bitcast.at_ref, ...), custom_call_target="tpu_custom_call" | custom-call | flops 1000000000 | bytes 4194304 | tf_op jit(solution)/shard_map/pallas_call | solution.py:228
  119.8 10.1 %collective-permute-start.15 = (bf16[16,16,512]{2,1,0:T(8,128)(2,1)}, bf16[16,16,512]{2,1,0:T(8,128)(2,1)S(1)}, u32[]{:S(2)}, u32[]{:S(2)}) collective-permute-start(bf16[16,16,512]{2,1,0:T(8,128)(2,1)} %get-tuple-element.169), channel_id=1, source_target_pairs={{0,8},{4,12},{8,16},{12,20},{16,24},{20,28},{24,0},{28,4},{1,9},{5... | collective-permute-start | bytes 786440 | tf_op jit(solution)/shard_map/ppermute | solution.py:307
  129.9 4.1 %collective-permute-start.16 = (bf16[16,16,512]{2,1,0:T(8,128)(2,1)}, bf16[16,16,512]{2,1,0:T(8,128)(2,1)S(1)}, u32[]{:S(2)}, u32[]{:S(2)}) collective-permute-start(bf16[16,16,512]{2,1,0:T(8,128)(2,1)} %get-tuple-element.170), channel_id=1, source_target_pairs={{0,12},{4,16},{8,20},{12,24},{16,28},{20,0},{24,4},{28,8},{1,13},{... | collective-permute-start | bytes 786440 | tf_op jit(solution)/shard_map/ppermute | solution.py:307
  134.0 4.4 %collective-permute-start.17 = (bf16[16,16,512]{2,1,0:T(8,128)(2,1)}, bf16[16,16,512]{2,1,0:T(8,128)(2,1)S(1)}, u32[]{:S(2)}, u32[]{:S(2)}) collective-permute-start(bf16[16,16,512]{2,1,0:T(8,128)(2,1)} %get-tuple-element.171), channel_id=1, source_target_pairs={{0,16},{4,20},{8,24},{12,28},{16,0},{20,4},{24,8},{28,12},{1,17},{... | collective-permute-start | bytes 786440 | tf_op jit(solution)/shard_map/ppermute | solution.py:307
  138.4 13.2 %collective-permute-start.18 = (bf16[16,16,512]{2,1,0:T(8,128)(2,1)}, bf16[16,16,512]{2,1,0:T(8,128)(2,1)S(1)}, u32[]{:S(2)}, u32[]{:S(2)}) collective-permute-start(bf16[16,16,512]{2,1,0:T(8,128)(2,1)} %get-tuple-element.172), channel_id=1, source_target_pairs={{0,20},{4,24},{8,28},{12,0},{16,4},{20,8},{24,12},{28,16},{1,21},{... | collective-permute-start | bytes 786440 | tf_op jit(solution)/shard_map/ppermute | solution.py:307
  153.4 28.2 %shard_map.211 = (bf16[32,16,256]{2,1,0:T(8,128)(2,1)}, bf16[32,16,256]{2,1,0:T(8,128)(2,1)}, bf16[32,16,256]{2,1,0:T(8,128)(2,1)}, bf16[32,16,256]{2,1,0:T(8,12...) custom-call(f32[384,640]{1,0:T(8,128)} %broadcast_in_dim.26.refs_0_,, ...), custom_call_target="tpu_custom_call" | custom-call | flops 30000001024 | bytes 4194304 | tf_op jit(solution)/shard_map/pallas_call | solution.py:228
  181.6 3.5 collective-permute-start.19
  185.4 13.2 %shard_map.212 = (bf16[16,16,512]{2,1,0:T(8,128)(2,1)}, bf16[16,16,512]{2,1,0:T(8,128)(2,1)}, bf16[16,16,512]{2,1,0:T(8,128)(2,1)}, bf16[16,16,512]{2,1,0:T(8,12...) custom-call(bf16[256,512]{1,0:T(8,128)(2,1)} %bitcast.115, ...), custom_call_target="tpu_custom_call" | custom-call | flops 10000000000 | bytes 4194304 | tf_op jit(solution)/shard_map/pallas_call | solution.py:228
  200.7 3.0 collective-permute-start.31
  204.5 28.3 %shard_map.213 = (bf16[32,16,256]{2,1,0:T(8,128)(2,1)}, bf16[32,16,256]{2,1,0:T(8,128)(2,1)}, bf16[32,16,256]{2,1,0:T(8,128)(2,1)}, bf16[32,16,256]{2,1,0:T(8,12...) custom-call(f32[384,640]{1,0:T(8,128)} %get-tuple-element.156.refs_0, ...), custom_call_target="tpu_custom_call", output_to_operand_aliasing={{0}: (28, {}), {1}: (29, {}), {2}: (30, {}), {3}: (31, {}),... | custom-call | flops 30000001024 | bytes 4194304 | tf_op jit(solution)/shard_map/pallas_call | solution.py:228
  232.8 13.3 %shard_map.214 = (bf16[16,16,512]{2,1,0:T(8,128)(2,1)}, bf16[16,16,512]{2,1,0:T(8,128)(2,1)}, bf16[16,16,512]{2,1,0:T(8,128)(2,1)}, bf16[16,16,512]{2,1,0:T(8,12...) custom-call(bf16[256,512]{1,0:T(8,128)(2,1)} %bitcast.117, ...), custom_call_target="tpu_custom_call" | custom-call | flops 10000000000 | bytes 4194304 | tf_op jit(solution)/shard_map/pallas_call | solution.py:228
  251.4 3.0 collective-permute-start.44
  262.9 7.2 %collective-permute-done.43 = f32[8,12,642]{2,0,1:T(8,128)S(1)} collective-permute-done((f32[8,12,642]{2,0,1:T(8,128)S(1)}, f32[8,12,642]{2,0,1:T(8,128)S(1)}, u32[]{:S(2)}, u32[]{:S(2)}) %collective-permute-start.43) | collective-permute-done | bytes 246560 | tf_op jit(solution)/shard_map/ppermute | solution.py:420
  272.3 6.2 %shard_map.215.rest_8_ = f32[16,8,32,512]{3,2,1,0:T(8,128)} custom-call(s32[1]{0:T(128)} %bitcast.at_ref, f32[16,8,32,512]{3,2,1,0:T(8,128)} %bitcast.144, bf16[16,8,32,512]{3,2,1,0:T(8,128)(2,1)} %bitcast.94, f32[16,1,1]{2,1,0:T(1,128)} %reshape.478.ns_ref, bf16[16,16,512]{2,1,0:T(8,128)(2,1)} %get-tuple-element.200.rest_0_, ...), custom_call_target="tpu_custom_call" | custom-call | flops 10000000000 | bytes 4194304 | tf_op jit(solution)/shard_map/pallas_call | solution.py:228
  280.6 30.0 %collective-permute-done.23.rest_3_ = bf16[16,16,512]{2,1,0:T(8,128)(2,1)S(1)} collective-permute-done((bf16[16,16,512]{2,1,0:T(8,128)(2,1)}, bf16[16,16,512]{2,1,0:T(8,128)(2,1)S(1)}, u32[]{:S(2)}, u32[]{:S(2)}) %collective-permute-start.23) | collective-permute-done | bytes 262176 | tf_op jit(solution)/shard_map/ppermute | solution.py:307
  315.5 2.7 collective-permute-done.37.rest_3_
  318.2 2.6 collective-permute-done.38.rest_4_
  320.8 9.7 %collective-permute-done.39.rest_5_ = bf16[32,16,256]{2,1,0:T(8,128)(2,1)S(1)} collective-permute-done((bf16[32,16,256]{2,1,0:T(8,128)(2,1)S(1)}, bf16[32,16,256]{2,1,0:T(8,128)(2,1)S(1)}, u32[]{:S(2)}, u32[]{:S(2)}) %collective-permute-start.39) | collective-permute-done | bytes 262176 | tf_op jit(solution)/shard_map/ppermute | solution.py:307
  330.5 14.4 %collective-permute-start.27 = (bf16[16,16,512]{2,1,0:T(8,128)(2,1)S(1)}, bf16[16,16,512]{2,1,0:T(8,128)(2,1)S(1)}, u32[]{:S(2)}, u32[]{:S(2)}) collective-permute-start(bf16[16,16,512]{2,1,0:T(8,128)(2,1)S(1)} %copy-done.11), channel_id=1, source_target_pairs={{0,28},{4,0},{8,4},{12,8},{16,12},{20,16},{24,20},{28,24},{1,29},{... | collective-permute-start | bytes 786440 | tf_op jit(solution)/shard_map/ppermute | solution.py:307
  345.7 19.9 %shard_map.218 = f32[16,256,512]{2,1,0:T(8,128)} custom-call(f32[16,128,256]{2,1,0:T(8,128)} %shard_map.217.g_ref, f32[16,1,128]{2,1,0:T(1,128)} %get-tuple-element.261.c_ref, f32[16,1,128]{2,1,0:T(1,128)} %get-tuple-element.260.s_ref, f32[16,128,1]{2,1,0:T(8,128)} %exponential_multiply_fusion.d_ref, bf16[256,512]{1,0:T(8,128)(2,1)} %bitcast.118, ...), custom_call_target="tpu_custom_call" | custom-call | flops 20000000000 | bytes 4194304 | tf_op jit(solution)/shard_map/pallas_call | solution.py:228
  371.2 6.2 %shard_map.216 = f32[16,8,32,512]{3,2,1,0:T(8,128)} custom-call(s32[1]{0:T(128)} %bitcast.at_ref, f32[16,8,32,512]{3,2,1,0:T(8,128)} %bitcast.145, bf16[16,8,32,512]{3,2,1,0:T(8,128)(2,1)} %bitcast.95, f32[16,1,1]{2,1,0:T(1,128)} %reshape.478.ns_ref, bf16[16,16,512]{2,1,0:T(8,128)(2,1)} %get-tuple-element.192.rest_0_, ...), custom_call_target="tpu_custom_call", output_to_operand_aliasing={{}: (12, {})} | custom-call | flops 10000000000 | bytes 4194304 | tf_op jit(solution)/shard_map/pallas_call | solution.py:228
  (250 shorter events, 53.3 us)
Async XLA Ops:
  42.6 31.0 %collective-permute-start.2 = (bf16[32,16,256]{2,1,0:T(8,128)(2,1)}, bf16[32,16,256]{2,1,0:T(8,128)(2,1)S(1)}, u32[]{:S(2)}, u32[]{:S(2)}) collective-permute-start(bf16[32,16,256]{2,1,0:T(8,128)(2,1)} %get-tuple-element.136), channel_id=1, source_target_pairs={{0,12},{4,16},{8,20},{12,24},{16,28},{20,0},{24,4},{28,8},{1,13},{... | collective-permute-start | bytes 786440 | tf_op jit(solution)/shard_map/ppermute | solution.py:307
  45.2 28.7 %collective-permute-start.3 = (bf16[32,16,256]{2,1,0:T(8,128)(2,1)}, bf16[32,16,256]{2,1,0:T(8,128)(2,1)S(1)}, u32[]{:S(2)}, u32[]{:S(2)}) collective-permute-start(bf16[32,16,256]{2,1,0:T(8,128)(2,1)} %get-tuple-element.137), channel_id=1, source_target_pairs={{0,16},{4,20},{8,24},{12,28},{16,0},{20,4},{24,8},{28,12},{1,17},{... | collective-permute-start | bytes 786440 | tf_op jit(solution)/shard_map/ppermute | solution.py:307
  46.4 38.8 %collective-permute-start.4 = (bf16[32,16,256]{2,1,0:T(8,128)(2,1)}, bf16[32,16,256]{2,1,0:T(8,128)(2,1)S(1)}, u32[]{:S(2)}, u32[]{:S(2)}) collective-permute-start(bf16[32,16,256]{2,1,0:T(8,128)(2,1)} %get-tuple-element.138), channel_id=1, source_target_pairs={{0,20},{4,24},{8,28},{12,0},{16,4},{20,8},{24,12},{28,16},{1,21},{... | collective-permute-start | bytes 786440 | tf_op jit(solution)/shard_map/ppermute | solution.py:307
  62.1 27.2 %collective-permute-start.5 = (bf16[32,16,256]{2,1,0:T(8,128)(2,1)}, bf16[32,16,256]{2,1,0:T(8,128)(2,1)S(1)}, u32[]{:S(2)}, u32[]{:S(2)}) collective-permute-start(bf16[32,16,256]{2,1,0:T(8,128)(2,1)} %get-tuple-element.139), channel_id=1, source_target_pairs={{0,24},{4,28},{8,0},{12,4},{16,8},{20,12},{24,16},{28,20},{1,25},{... | collective-permute-start | bytes 786440 | tf_op jit(solution)/shard_map/ppermute | solution.py:307
  63.5 29.7 %collective-permute-start.6 = (bf16[32,16,256]{2,1,0:T(8,128)(2,1)}, bf16[32,16,256]{2,1,0:T(8,128)(2,1)S(1)}, u32[]{:S(2)}, u32[]{:S(2)}) collective-permute-start(bf16[32,16,256]{2,1,0:T(8,128)(2,1)} %get-tuple-element.140), channel_id=1, source_target_pairs={{0,28},{4,0},{8,4},{12,8},{16,12},{20,16},{24,20},{28,24},{1,29},{... | collective-permute-start | bytes 786440 | tf_op jit(solution)/shard_map/ppermute | solution.py:307
  73.6 33.1 %collective-permute-start.7 = (bf16[16,16,512]{2,1,0:T(8,128)(2,1)}, bf16[16,16,512]{2,1,0:T(8,128)(2,1)}, u32[]{:S(2)}, u32[]{:S(2)}) collective-permute-start(bf16[16,16,512]{2,1,0:T(8,128)(2,1)} %get-tuple-element.149), channel_id=1, source_target_pairs={{0,4},{4,8},{8,12},{12,16},{16,20},{20,24},{24,28},{28,0},{1,5},{5... | collective-permute-start | bytes 786440 | tf_op jit(solution)/shard_map/ppermute | solution.py:307
  73.8 36.0 %collective-permute-start.8 = (bf16[16,16,512]{2,1,0:T(8,128)(2,1)}, bf16[16,16,512]{2,1,0:T(8,128)(2,1)}, u32[]{:S(2)}, u32[]{:S(2)}) collective-permute-start(bf16[16,16,512]{2,1,0:T(8,128)(2,1)} %get-tuple-element.150), channel_id=1, source_target_pairs={{0,8},{4,12},{8,16},{12,20},{16,24},{20,28},{24,0},{28,4},{1,9},{5... | collective-permute-start | bytes 786440 | tf_op jit(solution)/shard_map/ppermute | solution.py:307
  85.2 34.1 %collective-permute-start.9 = (bf16[16,16,512]{2,1,0:T(8,128)(2,1)}, bf16[16,16,512]{2,1,0:T(8,128)(2,1)}, u32[]{:S(2)}, u32[]{:S(2)}) collective-permute-start(bf16[16,16,512]{2,1,0:T(8,128)(2,1)} %get-tuple-element.151), channel_id=1, source_target_pairs={{0,12},{4,16},{8,20},{12,24},{16,28},{20,0},{24,4},{28,8},{1,13},{... | collective-permute-start | bytes 786440 | tf_op jit(solution)/shard_map/ppermute | solution.py:307
  89.4 30.4 %collective-permute-start.10 = (bf16[16,16,512]{2,1,0:T(8,128)(2,1)}, bf16[16,16,512]{2,1,0:T(8,128)(2,1)}, u32[]{:S(2)}, u32[]{:S(2)}) collective-permute-start(bf16[16,16,512]{2,1,0:T(8,128)(2,1)} %get-tuple-element.152), channel_id=1, source_target_pairs={{0,16},{4,20},{8,24},{12,28},{16,0},{20,4},{24,8},{28,12},{1,17},{... | collective-permute-start | bytes 786440 | tf_op jit(solution)/shard_map/ppermute | solution.py:307
  93.3 36.6 %collective-permute-start.11 = (bf16[16,16,512]{2,1,0:T(8,128)(2,1)}, bf16[16,16,512]{2,1,0:T(8,128)(2,1)}, u32[]{:S(2)}, u32[]{:S(2)}) collective-permute-start(bf16[16,16,512]{2,1,0:T(8,128)(2,1)} %get-tuple-element.153), channel_id=1, source_target_pairs={{0,20},{4,24},{8,28},{12,0},{16,4},{20,8},{24,12},{28,16},{1,21},{... | collective-permute-start | bytes 786440 | tf_op jit(solution)/shard_map/ppermute | solution.py:307
  106.7 27.3 %collective-permute-start.12 = (bf16[16,16,512]{2,1,0:T(8,128)(2,1)S(1)}, bf16[16,16,512]{2,1,0:T(8,128)(2,1)}, u32[]{:S(2)}, u32[]{:S(2)}) collective-permute-start(bf16[16,16,512]{2,1,0:T(8,128)(2,1)S(1)} %copy-done.24), channel_id=1, source_target_pairs={{0,24},{4,28},{8,0},{12,4},{16,8},{20,12},{24,16},{28,20},{1,25},{... | collective-permute-start | bytes 786440 | tf_op jit(solution)/shard_map/ppermute | solution.py:307
  109.8 28.6 %collective-permute-start.13 = (bf16[16,16,512]{2,1,0:T(8,128)(2,1)S(1)}, bf16[16,16,512]{2,1,0:T(8,128)(2,1)}, u32[]{:S(2)}, u32[]{:S(2)}) collective-permute-start(bf16[16,16,512]{2,1,0:T(8,128)(2,1)S(1)} %copy-done.23), channel_id=1, source_target_pairs={{0,28},{4,0},{8,4},{12,8},{16,12},{20,16},{24,20},{28,24},{1,29},{... | collective-permute-start | bytes 786440 | tf_op jit(solution)/shard_map/ppermute | solution.py:307
  119.3 62.3 %collective-permute-start.14 = (bf16[16,16,512]{2,1,0:T(8,128)(2,1)}, bf16[16,16,512]{2,1,0:T(8,128)(2,1)S(1)}, u32[]{:S(2)}, u32[]{:S(2)}) collective-permute-start(bf16[16,16,512]{2,1,0:T(8,128)(2,1)} %get-tuple-element.168), channel_id=1, source_target_pairs={{0,4},{4,8},{8,12},{12,16},{16,20},{20,24},{24,28},{28,0},{1,5},{5... | collective-permute-start | bytes 786440 | tf_op jit(solution)/shard_map/ppermute | solution.py:307
  119.8 65.3 %collective-permute-start.15 = (bf16[16,16,512]{2,1,0:T(8,128)(2,1)}, bf16[16,16,512]{2,1,0:T(8,128)(2,1)S(1)}, u32[]{:S(2)}, u32[]{:S(2)}) collective-permute-start(bf16[16,16,512]{2,1,0:T(8,128)(2,1)} %get-tuple-element.169), channel_id=1, source_target_pairs={{0,8},{4,12},{8,16},{12,20},{16,24},{20,28},{24,0},{28,4},{1,9},{5... | collective-permute-start | bytes 786440 | tf_op jit(solution)/shard_map/ppermute | solution.py:307
  129.9 68.7 %collective-permute-start.16 = (bf16[16,16,512]{2,1,0:T(8,128)(2,1)}, bf16[16,16,512]{2,1,0:T(8,128)(2,1)S(1)}, u32[]{:S(2)}, u32[]{:S(2)}) collective-permute-start(bf16[16,16,512]{2,1,0:T(8,128)(2,1)} %get-tuple-element.170), channel_id=1, source_target_pairs={{0,12},{4,16},{8,20},{12,24},{16,28},{20,0},{24,4},{28,8},{1,13},{... | collective-permute-start | bytes 786440 | tf_op jit(solution)/shard_map/ppermute | solution.py:307
  134.0 65.1 %collective-permute-start.17 = (bf16[16,16,512]{2,1,0:T(8,128)(2,1)}, bf16[16,16,512]{2,1,0:T(8,128)(2,1)S(1)}, u32[]{:S(2)}, u32[]{:S(2)}) collective-permute-start(bf16[16,16,512]{2,1,0:T(8,128)(2,1)} %get-tuple-element.171), channel_id=1, source_target_pairs={{0,16},{4,20},{8,24},{12,28},{16,0},{20,4},{24,8},{28,12},{1,17},{... | collective-permute-start | bytes 786440 | tf_op jit(solution)/shard_map/ppermute | solution.py:307
  138.4 61.6 %collective-permute-start.18 = (bf16[16,16,512]{2,1,0:T(8,128)(2,1)}, bf16[16,16,512]{2,1,0:T(8,128)(2,1)S(1)}, u32[]{:S(2)}, u32[]{:S(2)}) collective-permute-start(bf16[16,16,512]{2,1,0:T(8,128)(2,1)} %get-tuple-element.172), channel_id=1, source_target_pairs={{0,20},{4,24},{8,28},{12,0},{16,4},{20,8},{24,12},{28,16},{1,21},{... | collective-permute-start | bytes 786440 | tf_op jit(solution)/shard_map/ppermute | solution.py:307
  198.6 48.3 %collective-permute-start.28 = (bf16[16,16,512]{2,1,0:T(8,128)(2,1)}, bf16[16,16,512]{2,1,0:T(8,128)(2,1)S(1)}, u32[]{:S(2)}, u32[]{:S(2)}) collective-permute-start(bf16[16,16,512]{2,1,0:T(8,128)(2,1)} %get-tuple-element.201), channel_id=1, source_target_pairs={{0,4},{4,8},{8,12},{12,16},{16,20},{20,24},{24,28},{28,0},{1,5},{5... | collective-permute-start | bytes 786440 | tf_op jit(solution)/shard_map/ppermute | solution.py:307
  199.2 51.2 %collective-permute-start.29 = (bf16[16,16,512]{2,1,0:T(8,128)(2,1)}, bf16[16,16,512]{2,1,0:T(8,128)(2,1)}, u32[]{:S(2)}, u32[]{:S(2)}) collective-permute-start(bf16[16,16,512]{2,1,0:T(8,128)(2,1)} %get-tuple-element.202), channel_id=1, source_target_pairs={{0,8},{4,12},{8,16},{12,20},{16,24},{20,28},{24,0},{28,4},{1,9},{5... | collective-permute-start | bytes 786440 | tf_op jit(solution)/shard_map/ppermute | solution.py:307
  200.0 51.4 %collective-permute-start.30 = (bf16[16,16,512]{2,1,0:T(8,128)(2,1)}, bf16[16,16,512]{2,1,0:T(8,128)(2,1)}, u32[]{:S(2)}, u32[]{:S(2)}) collective-permute-start(bf16[16,16,512]{2,1,0:T(8,128)(2,1)} %get-tuple-element.203), channel_id=1, source_target_pairs={{0,12},{4,16},{8,20},{12,24},{16,28},{20,0},{24,4},{28,8},{1,13},{... | collective-permute-start | bytes 786440 | tf_op jit(solution)/shard_map/ppermute | solution.py:307
  200.7 50.7 %collective-permute-start.31 = (bf16[16,16,512]{2,1,0:T(8,128)(2,1)}, bf16[16,16,512]{2,1,0:T(8,128)(2,1)}, u32[]{:S(2)}, u32[]{:S(2)}) collective-permute-start(bf16[16,16,512]{2,1,0:T(8,128)(2,1)} %get-tuple-element.204), channel_id=1, source_target_pairs={{0,16},{4,20},{8,24},{12,28},{16,0},{20,4},{24,8},{28,12},{1,17},{... | collective-permute-start | bytes 786440 | tf_op jit(solution)/shard_map/ppermute | solution.py:307
  203.7 50.7 %collective-permute-start.32 = (bf16[16,16,512]{2,1,0:T(8,128)(2,1)}, bf16[16,16,512]{2,1,0:T(8,128)(2,1)}, u32[]{:S(2)}, u32[]{:S(2)}) collective-permute-start(bf16[16,16,512]{2,1,0:T(8,128)(2,1)} %get-tuple-element.205), channel_id=1, source_target_pairs={{0,20},{4,24},{8,28},{12,0},{16,4},{20,8},{24,12},{28,16},{1,21},{... | collective-permute-start | bytes 786440 | tf_op jit(solution)/shard_map/ppermute | solution.py:307
  261.9 48.8 %collective-permute-start.23 = (bf16[16,16,512]{2,1,0:T(8,128)(2,1)}, bf16[16,16,512]{2,1,0:T(8,128)(2,1)S(1)}, u32[]{:S(2)}, u32[]{:S(2)}) collective-permute-start(bf16[16,16,512]{2,1,0:T(8,128)(2,1)} %get-tuple-element.195), channel_id=1, source_target_pairs={{0,12},{4,16},{8,20},{12,24},{16,28},{20,0},{24,4},{28,8},{1,13},{... | collective-permute-start | bytes 786440 | tf_op jit(solution)/shard_map/ppermute | solution.py:307
  270.2 41.1 %collective-permute-start.24 = (bf16[16,16,512]{2,1,0:T(8,128)(2,1)}, bf16[16,16,512]{2,1,0:T(8,128)(2,1)S(1)}, u32[]{:S(2)}, u32[]{:S(2)}) collective-permute-start(bf16[16,16,512]{2,1,0:T(8,128)(2,1)} %get-tuple-element.196), channel_id=1, source_target_pairs={{0,16},{4,20},{8,24},{12,28},{16,0},{20,4},{24,8},{28,12},{1,17},{... | collective-permute-start | bytes 786440 | tf_op jit(solution)/shard_map/ppermute | solution.py:307
  271.2 42.0 %collective-permute-start.35 = (bf16[32,16,256]{2,1,0:T(8,128)(2,1)}, bf16[32,16,256]{2,1,0:T(8,128)(2,1)S(1)}, u32[]{:S(2)}, u32[]{:S(2)}) collective-permute-start(bf16[32,16,256]{2,1,0:T(8,128)(2,1)} %get-tuple-element.209), channel_id=1, source_target_pairs={{0,4},{4,8},{8,12},{12,16},{16,20},{20,24},{24,28},{28,0},{1,5},{5... | collective-permute-start | bytes 786440 | tf_op jit(solution)/shard_map/ppermute | solution.py:307
  271.2 42.0 %collective-permute-start.36 = (bf16[32,16,256]{2,1,0:T(8,128)(2,1)}, bf16[32,16,256]{2,1,0:T(8,128)(2,1)S(1)}, u32[]{:S(2)}, u32[]{:S(2)}) collective-permute-start(bf16[32,16,256]{2,1,0:T(8,128)(2,1)} %get-tuple-element.210), channel_id=1, source_target_pairs={{0,8},{4,12},{8,16},{12,20},{16,24},{20,28},{24,0},{28,4},{1,9},{5... | collective-permute-start | bytes 786440 | tf_op jit(solution)/shard_map/ppermute | solution.py:307
  278.5 39.6 %collective-permute-start.37 = (bf16[32,16,256]{2,1,0:T(8,128)(2,1)S(1)}, bf16[32,16,256]{2,1,0:T(8,128)(2,1)S(1)}, u32[]{:S(2)}, u32[]{:S(2)}) collective-permute-start(bf16[32,16,256]{2,1,0:T(8,128)(2,1)S(1)} %copy-done.41), channel_id=1, source_target_pairs={{0,12},{4,16},{8,20},{12,24},{16,28},{20,0},{24,4},{28,8},{1,13},{... | collective-permute-start | bytes 786440 | tf_op jit(solution)/shard_map/ppermute | solution.py:307
  313.2 31.8 %collective-permute-start.40 = (bf16[32,16,256]{2,1,0:T(8,128)(2,1)S(1)}, bf16[32,16,256]{2,1,0:T(8,128)(2,1)S(1)}, u32[]{:S(2)}, u32[]{:S(2)}) collective-permute-start(bf16[32,16,256]{2,1,0:T(8,128)(2,1)S(1)} %copy-done.44), channel_id=1, source_target_pairs={{0,24},{4,28},{8,0},{12,4},{16,8},{20,12},{24,16},{28,20},{1,25},{... | collective-permute-start | bytes 786440 | tf_op jit(solution)/shard_map/ppermute | solution.py:307
  313.3 31.8 %collective-permute-start.41 = (bf16[32,16,256]{2,1,0:T(8,128)(2,1)S(1)}, bf16[32,16,256]{2,1,0:T(8,128)(2,1)S(1)}, u32[]{:S(2)}, u32[]{:S(2)}) collective-permute-start(bf16[32,16,256]{2,1,0:T(8,128)(2,1)S(1)} %copy-done.45), channel_id=1, source_target_pairs={{0,28},{4,0},{8,4},{12,8},{16,12},{20,16},{24,20},{28,24},{1,29},{... | collective-permute-start | bytes 786440 | tf_op jit(solution)/shard_map/ppermute | solution.py:307
  318.2 47.5 %collective-permute-start.25 = (bf16[16,16,512]{2,1,0:T(8,128)(2,1)S(1)}, bf16[16,16,512]{2,1,0:T(8,128)(2,1)S(1)}, u32[]{:S(2)}, u32[]{:S(2)}) collective-permute-start(bf16[16,16,512]{2,1,0:T(8,128)(2,1)S(1)} %copy-done.13), channel_id=1, source_target_pairs={{0,20},{4,24},{8,28},{12,0},{16,4},{20,8},{24,12},{28,16},{1,21},{... | collective-permute-start | bytes 786440 | tf_op jit(solution)/shard_map/ppermute | solution.py:307
  320.8 47.2 %collective-permute-start.26 = (bf16[16,16,512]{2,1,0:T(8,128)(2,1)S(1)}, bf16[16,16,512]{2,1,0:T(8,128)(2,1)S(1)}, u32[]{:S(2)}, u32[]{:S(2)}) collective-permute-start(bf16[16,16,512]{2,1,0:T(8,128)(2,1)S(1)} %copy-done.12), channel_id=1, source_target_pairs={{0,24},{4,28},{8,0},{12,4},{16,8},{20,12},{24,16},{28,20},{1,25},{... | collective-permute-start | bytes 786440 | tf_op jit(solution)/shard_map/ppermute | solution.py:307
  330.5 38.2 %collective-permute-start.27 = (bf16[16,16,512]{2,1,0:T(8,128)(2,1)S(1)}, bf16[16,16,512]{2,1,0:T(8,128)(2,1)S(1)}, u32[]{:S(2)}, u32[]{:S(2)}) collective-permute-start(bf16[16,16,512]{2,1,0:T(8,128)(2,1)S(1)} %copy-done.11), channel_id=1, source_target_pairs={{0,28},{4,0},{8,4},{12,8},{16,12},{20,16},{24,20},{28,24},{1,29},{... | collective-permute-start | bytes 786440 | tf_op jit(solution)/shard_map/ppermute | solution.py:307
  (74 other events, 2049.8 us)
